TPU v7x, 32 devices: a 4x4x1 block of a 4x4x8 slice. The times are simulated.
32 devices in a mesh: dp: 1 (over z), tp: 4 (over y), ep: 8 (over x, core).
Axes of the slice: x: 4, y: 4, z: 1, core: 2. Of those that a mesh axis runs over, the one named last changes fastest.
The devices are a block of a 4x4x8 slice.
Arguments:
- resid_in: bfloat16 [2048, 4096], P(('dp', 'ep'))
- norm_scale: bfloat16 [4096], replicated
- w_router: bfloat16 [4096, 16], replicated
- w_gate: bfloat16 [16, 4096, 3072], P('ep', None, 'tp')
- w_up: bfloat16 [16, 4096, 3072], P('ep', None, 'tp')
- w_down: bfloat16 [16, 3072, 4096], P('ep', 'tp')
- choice: int32 [2048, 2], P(('dp', 'ep'))
Outputs:
- output: bfloat16 [2048, 4096], P(('dp', 'ep'))
All inputs are finite; a program needn't handle non-finite values.
Results may differ from a plain program's by a relative error of at most 0.00643143.
Values are sent between devices in bfloat16 or wider.
A program may use at most 768 MiB of HBM per device.

v0:
```python
import jax
import jax.numpy as jnp
from jax import lax
from jax.sharding import PartitionSpec as P

NORM_EPS = 1e-5


def norm_route(resid_rows, norm_scale, w_router, choice_rows):
    rows_f32 = resid_rows.astype(jnp.float32)
    centered = rows_f32 - jnp.mean(rows_f32, axis=-1, keepdims=True)
    variance = jnp.mean(centered * centered, axis=-1, keepdims=True)
    normed = (centered * lax.rsqrt(variance + NORM_EPS) * norm_scale.astype(jnp.float32)).astype(jnp.bfloat16)
    logits = jnp.dot(normed, w_router, preferred_element_type=jnp.float32)
    router_probs = jax.nn.softmax(logits, axis=-1)
    expert_ids = jnp.arange(w_router.shape[1], dtype=jnp.int32)
    picked = jnp.sum(jnp.where(choice_rows[:, :, None] == expert_ids[None, None, :], router_probs[:, None, :], 0.0), axis=-1)
    gate_vals = picked / jnp.sum(picked, axis=-1, keepdims=True)
    return normed, gate_vals


def slot_table(choice_rows, experts, capacity):
    flat_ids = choice_rows.reshape(-1)
    onehot = (flat_ids[:, None] == jnp.arange(experts, dtype=jnp.int32)[None, :]).astype(jnp.int32)
    earlier = jnp.cumsum(onehot, axis=0) - onehot
    position = jnp.sum(earlier * onehot, axis=1)
    return flat_ids * capacity + position, position < capacity


def slot_sources(slot_ids, is_kept, num_slots, top_k):
    slot_match = (slot_ids[None, :] == jnp.arange(num_slots, dtype=jnp.int32)[:, None]) & is_kept[None, :]
    token_rows = jnp.arange(slot_ids.shape[0], dtype=jnp.int32) // top_k
    source_row = jnp.sum(jnp.where(slot_match, token_rows[None, :], 0), axis=1)
    return source_row, jnp.any(slot_match, axis=1)


def expert_glu(rows_in, w_gate, w_up, w_down):
    gate_act = jnp.einsum('esd,edf->esf', rows_in, w_gate, preferred_element_type=jnp.float32)
    up_act = jnp.einsum('esd,edf->esf', rows_in, w_up, preferred_element_type=jnp.float32)
    hidden = (jax.nn.silu(gate_act) * up_act).astype(jnp.bfloat16)
    return jnp.einsum('esf,efd->esd', hidden, w_down, preferred_element_type=jnp.float32).astype(jnp.bfloat16)


def solution(mesh):
    row_spec = P(('dp', 'ep'), None)

    def device_step(resid_in, norm_scale, w_router, w_gate, w_up, w_down, choice):
        tok_rows, d_model = resid_in.shape
        experts = w_router.shape[1]
        top_k = choice.shape[1]
        capacity = (2 * tok_rows * top_k + experts - 1) // experts
        normed, gate_vals = norm_route(resid_in, norm_scale, w_router, choice)
        slot_ids, is_kept = slot_table(choice, experts, capacity)
        source_row, filled = slot_sources(slot_ids, is_kept, experts * capacity, top_k)
        send_rows = jnp.where(filled[:, None], jnp.take(normed, source_row, axis=0), jnp.zeros((), jnp.bfloat16))
        send_rows = send_rows.reshape(experts, capacity, d_model)
        expert_rows = lax.all_to_all(send_rows, 'ep', 0, 1, tiled=True)
        expert_out = expert_glu(expert_rows, w_gate, w_up, w_down)
        back_rows = lax.all_to_all(expert_out, 'ep', 1, 0, tiled=True).reshape(experts * capacity, d_model)
        kept_rows = is_kept.reshape(tok_rows, top_k)
        safe_slots = jnp.where(kept_rows, slot_ids.reshape(tok_rows, top_k), 0)
        weights = jnp.where(kept_rows, gate_vals, 0.0)
        picked_rows = jnp.take(back_rows, safe_slots, axis=0)
        mixed_rows = jnp.sum(weights[:, :, None] * picked_rows, axis=1)
        tp_total = lax.psum(mixed_rows, 'tp')
        return (resid_in.astype(jnp.float32) + tp_total).astype(jnp.bfloat16)

    return jax.shard_map(device_step, mesh=mesh, in_specs=(row_spec, P(None), P(None, None), P('ep', None, 'tp'), P('ep', None, 'tp'), P('ep', 'tp', None), row_spec), out_specs=row_spec, check_vma=False)
```

profile of v0, /device:TPU:97, one launch (start us, length us, event | category | flops | bytes accessed | tf_op | source)
XLA Modules:
  0.0 443.0 jit_solution(1653367219877163426)
XLA Ops:
  6.6 0.9 copy.32
  7.4 0.1 eq.51
  7.6 0.1 eq.55
  7.7 1.2 reduce-window.6
  8.9 0.2 slice_reduce_fusion
  9.3 2.0 convert_reduce_fusion
  11.2 2.3 fusion.2
  13.5 0.4 fusion.7
  13.9 0.5 select_reduce_fusion
  14.6 2.5 fusion.4
  17.1 7.7 %gather_fusion = bf16[1024,4096]{1,0:T(8,128)(2,1)} fusion(bf16[256,4096]{1,0:T(8,128)(2,1)S(1)} %fusion.4, s32[1024]{0:T(1024)S(1)} %broadcast_clamp_fusion), kind=kCustom, calls=%fused_computation | custom fusion | bytes 16781312 | tf_op jit(solution)/shard_map/jit(_take)/gather | solution.py:55
  24.8 4.7 %select_select_fusion = bf16[16,64,4096]{2,1,0:T(8,128)(2,1)S(1)} fusion(bf16[16,64,4096]{2,1,0:T(8,128)(2,1)} %bitcast.39, pred[16,64]{1,0:T(8,128)(4,1)S(1)} %compare_and_fusion, pred[16,64]{1,0:T(8,128)(4,1)S(1)} %broadcast_in_dim.89), kind=kLoop, calls=%fused_computation.3 | loop fusion | flops 8388608 | bytes 16779264 | tf_op jit(solution)/shard_map/jit(_where)/select_n | solution.py:55
  29.5 99.4 %all_to_all.33 = bf16[16,64,4096]{2,1,0:T(8,128)(2,1)} all-to-all(bf16[16,64,4096]{2,1,0:T(8,128)(2,1)S(1)} %select_select_fusion), channel_id=1, replica_groups=mesh['dp'=1,'tp'=4,'ep'=8] {'ep'}, dimensions={0} | all-to-all | bytes 16777216 | tf_op jit(solution)/shard_map/all_to_all | solution.py:57
  128.9 7.7 %copy.39 = bf16[2,8,64,4096]{3,2,1,0:T(8,128)(2,1)} copy(bf16[2,8,64,4096]{3,2,0,1:T(8,128)(2,1)} %bitcast.40) | data formatting | bytes 16777216 | tf_op jit(solution)/shard_map/all_to_all | solution.py:57
  136.6 12.3 %fusion.18 = f32[2,512,768]{2,1,0:T(8,128)S(1)} fusion(bf16[2,512,4096]{2,1,0:T(8,128)(2,1)} %bitcast.41, bf16[2,4096,768]{2,1,0:T(8,128)(2,1)} %param.10), kind=kOutput, calls=%fused_computation.56 | convolution fusion | flops 6442450944 | bytes 24117248 | tf_op jit(solution)/shard_map/esd,edf->esf/dot_general | solution.py:38
  148.9 9.8 %multiply_convert_fusion = bf16[2,512,768]{2,1,0:T(8,128)(2,1)S(1)} fusion(f32[2,512,768]{2,1,0:T(8,128)S(1)} %fusion.18, bf16[2,512,4096]{2,1,0:T(8,128)(2,1)S(1)} %bitcast.42, bf16[2,4096,768]{2,1,0:T(8,128)(2,1)} %param.11), kind=kOutput, calls=%fused_computation.15 | convolution fusion | flops 6447169536 | bytes 25690112 | tf_op jit(solution)/shard_map/esd,edf->esf/dot_general | solution.py:39
  158.7 11.6 %convolution_convert_fusion = bf16[2,512,4096]{2,1,0:T(8,128)(2,1)S(1)} fusion(bf16[2,512,768]{2,1,0:T(8,128)(2,1)S(1)} %multiply_convert_fusion, bf16[2,768,4096]{2,1,0:T(8,128)(2,1)} %param.12), kind=kOutput, calls=%fused_computation.5 | convolution fusion | flops 6446645248 | bytes 22544384 | tf_op jit(solution)/shard_map/esf,efd->esd/dot_general | solution.py:41
  170.3 22.3 %copy.40 = bf16[2,512,4096]{2,0,1:T(2,128)(2,1)} copy(bf16[2,512,4096]{2,1,0:T(8,128)(2,1)S(1)} %convolution_convert_fusion) | data formatting | bytes 16777216 | tf_op jit(solution)/shard_map/convert_element_type | solution.py:41
  192.7 6.1 %all-to-all-start.1 = ((bf16[2,512,4096]{2,0,1:T(2,128)(2,1)}), bf16[2,512,4096]{2,0,1:T(2,128)(2,1)}, u32[]{:S(2)}, u32[]{:S(2)}) async-start(bf16[2,512,4096]{2,0,1:T(2,128)(2,1)} %copy.40), calls=%async_computation.1 | async-start | bytes 16777216 | tf_op jit(solution)/shard_map/all_to_all | solution.py:59
  198.7 0.1 reduce_sum.79
  199.0 0.2 copy.38
  199.2 0.1 copy.42
  199.3 0.1 reshape.139
  199.5 0.7 fusion.17
  200.2 0.1 copy.36
  200.4 92.0 %all-to-all-done.1 = bf16[2,512,4096]{2,0,1:T(2,128)(2,1)} async-done(((bf16[2,512,4096]{2,0,1:T(2,128)(2,1)}), bf16[2,512,4096]{2,0,1:T(2,128)(2,1)}, u32[]{:S(2)}, u32[]{:S(2)}) %all-to-all-start.1) | async-done | bytes 8388640 | tf_op jit(solution)/shard_map/all_to_all | solution.py:59
  292.3 12.6 %copy.41 = bf16[2,8,64,4096]{3,2,0,1:T(8,128)(2,1)} copy(bf16[2,8,64,4096]{3,0,2,1:T(2,128)(2,1)} %bitcast.7) | data formatting | bytes 16777216 | tf_op jit(solution)/shard_map/all_to_all | solution.py:59
  305.0 13.3 %gather_fusion.1 = bf16[512,4096]{1,0:T(8,128)(2,1)} fusion(bf16[1024,4096]{1,0:T(8,128)(2,1)} %bitcast.38, s32[1024]{0:T(1024)S(1)} %pad_clamp_fusion), kind=kCustom, calls=%fused_computation.1 | custom fusion | bytes 8390656 | tf_op jit(solution)/shard_map/jit(_take)/gather | solution.py:63
  318.3 7.6 %reshape.138 = bf16[256,2,4096]{2,1,0:T(2,128)(2,1)} reshape(bf16[512,4096]{1,0:T(8,128)(2,1)} %gather_fusion.1) | data formatting | bytes 8388608 | tf_op jit(solution)/shard_map/jit(_take)/gather | solution.py:63
  325.9 17.3 %multiply_reduce_fusion = f32[256,4096]{1,0:T(8,128)} fusion(bf16[256,2,4096]{2,1,0:T(2,128)(2,1)} %reshape.138, pred[256,2]{1,0:T(8,128)(4,1)S(1)} %copy.38, f32[256,2]{1,0:T(8,128)S(1)} %copy.36), kind=kLoop, calls=%fused_computation.2 | loop fusion | flops 7340032 | bytes 8391168 | tf_op jit(solution)/shard_map/reduce_sum | solution.py:64
  343.2 88.8 %all-reduce.2.cloned.1.call-done = f32[256,4096]{1,0:T(8,128)} async-done(((f32[256,4096]{1,0:T(8,128)}), f32[256,4096]{1,0:T(8,128)}) %all-reduce.2.cloned.1.call-update) | async-done | bytes 4194320 | tf_op jit(solution)/shard_map/psum | solution.py:65
  432.0 4.1 fusion.5
  (33 shorter events, 0.6 us)
Async XLA Ops:
  6.5 192.9 %copy-start = (bf16[4096,16]{0,1:T(8,128)(2,1)S(1)}, bf16[4096,16]{0,1:T(8,128)(2,1)}, u32[]{:S(2)}) copy-start(bf16[4096,16]{0,1:T(8,128)(2,1)} %param.9) | copy-start | bytes 393220
  6.6 7.0 %copy-start.4 = (bf16[4096]{0:T(1024)(128)(2,1)S(1)}, bf16[4096]{0:T(1024)(128)(2,1)}, u32[]{:S(2)}) copy-start(bf16[4096]{0:T(1024)(128)(2,1)} %param.8) | copy-start | bytes 24580
  136.6 12.3 %copy-start.2 = (bf16[2,8,64,4096]{3,2,1,0:T(8,128)(2,1)S(1)}, bf16[2,8,64,4096]{3,2,1,0:T(8,128)(2,1)}, u32[]{:S(2)}) copy-start(bf16[2,8,64,4096]{3,2,1,0:T(8,128)(2,1)} %copy.39) | copy-start | bytes 25165828
  192.6 6.3 %copy-start.3 = (s32[256,2]{0,1:T(2,128)S(1)}, s32[256,2]{0,1:T(2,128)}, u32[]{:S(2)}) copy-start(s32[256,2]{0,1:T(2,128)} %param.13) | copy-start | bytes 6148
  192.7 99.7 %all-to-all-start.1 = ((bf16[2,512,4096]{2,0,1:T(2,128)(2,1)}), bf16[2,512,4096]{2,0,1:T(2,128)(2,1)}, u32[]{:S(2)}, u32[]{:S(2)}) async-start(bf16[2,512,4096]{2,0,1:T(2,128)(2,1)} %copy.40), calls=%async_computation.1 | async-start | bytes 16777216 | tf_op jit(solution)/shard_map/all_to_all | solution.py:59
  198.7 233.3 %all-reduce.2.cloned.1.call-start = ((), (), s32[]{:S(2)}) async-start(), calls=%async_computation.2 | async-start | bytes 8388608 | tf_op jit(solution)/shard_map/psum | solution.py:65
  343.2 88.9 %copy-start.1 = (bf16[256,4096]{1,0:T(8,128)(2,1)S(1)}, bf16[256,4096]{1,0:T(8,128)(2,1)}, u32[]{:S(2)}) copy-start(bf16[256,4096]{1,0:T(8,128)(2,1)} %param.7) | copy-start | bytes 6291460
Sparse Core Ops, SparseCore 0:
  343.3 88.6 all-reduce.1
where the time goes:
time: 444 us; the launch traced here: 443 us
  waiting for transfers between devices  181 us (41%)
  blocking collectives  99.4 us (22%)
  local copies, waits for them, and re-layouts  73.6 us (17%)
  other arithmetic  35 us (8%)
  matrix products  34.4 us (8%)
  between operations  13.6 us (3%)
  starting transfers between devices  6.09 us (1%)
    all_to_all x1, blocking collectives, device_step(): expert_rows = lax.all_to_all(send_rows, 'ep', 0, 1, tiled=True)  99.4 us
    all_to_all x1, waiting for transfers between devices, device_step(): lax.all_to_all(expert_out, 'ep', 1, 0, tiled=True)  92 us
    psum x1, waiting for transfers between devices, device_step(): tp_total = lax.psum(mixed_rows, 'tp')  88.8 us
    convert_element_type x1, local copies, waits for them, and re-layouts, expert_glu(): jnp.einsum('esf,efd->esd', hidden, w_down, preferred_element_type=jnp.flo...  22.3 us
    gather x2, local copies, waits for them, and re-layouts, device_step(): picked_rows = jnp.take(back_rows, safe_slots, axis=0)  20.9 us
    reduce_sum x1, other arithmetic, device_step(): mixed_rows = jnp.sum(weights[:, :, None] * picked_rows, axis=1)  17.3 us
    all_to_all x1, local copies, waits for them, and re-layouts, device_step(): lax.all_to_all(expert_out, 'ep', 1, 0, tiled=True)  12.6 us
    dot_general x1, matrix products, expert_glu(): jnp.einsum('esd,edf->esf', rows_in, w_gate, preferred_element_type=jnp.fl...  12.3 us
  transfers between devices with their start and end apart: 2, of which 2 were waited for; matrix products, arithmetic and copies ran while one was open for 0% of the time, Pallas kernels for 0%

commit v1 on v0

v1 whole, which is shorter than its diff:
```python
import functools

import jax
import jax.numpy as jnp
from jax import lax
from jax.experimental import pallas as pl
from jax.experimental.pallas import tpu as pltpu
from jax.sharding import PartitionSpec as P

NORM_EPS = 1e-5
MESH = pl.DeviceIdType.MESH
BF16 = jnp.bfloat16
F32 = jnp.float32
SUBS = 4


def norm_route(resid_rows, norm_scale, w_router, choice_rows):
    rows_f32 = resid_rows.astype(F32)
    centered = rows_f32 - jnp.mean(rows_f32, axis=-1, keepdims=True)
    variance = jnp.mean(centered * centered, axis=-1, keepdims=True)
    normed = (centered * lax.rsqrt(variance + NORM_EPS) * norm_scale.astype(F32)).astype(BF16)
    logits = jnp.dot(normed, w_router, preferred_element_type=F32)
    router_probs = jax.nn.softmax(logits, axis=-1)
    expert_ids = jnp.arange(w_router.shape[1], dtype=jnp.int32)
    chosen = choice_rows[:, :, None] == expert_ids[None, None, :]
    picked = jnp.sum(jnp.where(chosen, router_probs[:, None, :], 0.0), axis=-1)
    gate_vals = picked / jnp.sum(picked, axis=-1, keepdims=True)
    gate_by_expert = jnp.sum(jnp.where(chosen, gate_vals[:, :, None], 0.0), axis=1)
    return normed, gate_by_expert, jnp.any(chosen, axis=1)


def slot_meta(gate_by_expert, is_chosen, capacity):
    rows = is_chosen.shape[0]
    earlier = jnp.arange(rows)[:, None] > jnp.arange(rows)[None, :]
    position = jnp.dot(earlier.astype(BF16), is_chosen.astype(BF16), preferred_element_type=F32)
    kept = is_chosen & (position < capacity)
    return jnp.concatenate([jnp.where(kept, position, -1.0).T, jnp.where(kept, gate_by_expert, 0.0).T], axis=0)


def moe_kernel(experts, capacity, ny, nx, u_in, resid, meta_in, w_gate, w_up, w_down, out, ug,
               w1, v1, w2, xg, hid, hpart, sums, rfar, rplus, rminus, yown, yfar, yplus, yminus, fin, xres, utile, gsplit, meta,
               load_sem, tile_sem, send_sem, recv_sem):
    rows, d_model = resid.shape
    half = d_model // 2
    quarter = half // ny
    width = w_gate.shape[2]
    chunk = rows // 8
    sub = rows // SUBS
    tile = utile.shape[2]
    y = lax.axis_index('tp')
    ep = lax.axis_index('ep')
    core = lax.rem(ep, 2)
    x = ep // 2

    def ep_at(dx, other=False):
        return lax.rem(x + dx + nx, nx) * 2 + ((1 - core) if other else core)

    def dev_x(dx, other=False):
        return {'ep': ep_at(dx, other)}

    def dev_y(dy, other=False):
        return {'tp': lax.rem(y + dy + ny, ny), 'ep': ep_at(0, other)}

    partner = dev_x(0, True)

    barrier = pltpu.get_barrier_semaphore()
    peers = [dev_x(dx, o) for dx in range(nx) for o in (False, True) if (dx, o) != (0, False)]
    peers += [dev_y(dy, o) for dy in (1, -1) for o in (False, True)]
    for peer in peers:
        pl.semaphore_signal(barrier, inc=1, device_id=peer, device_id_type=MESH)
    pl.semaphore_wait(barrier, len(peers))

    copies = []

    def remote(src, dst, device):
        at = len(copies)
        copy = pltpu.make_async_remote_copy(src_ref=src, dst_ref=dst, send_sem=send_sem.at[at], recv_sem=recv_sem.at[at], device_id=device, device_id_type=MESH)
        copies.append(copy)
        copy.start()
        return copy

    sent = []

    def finish_send(copy):
        copy.wait_send()
        sent.append(copy)

    locals_ = []

    def local(src, dst):
        copy = pltpu.make_async_copy(src, dst, load_sem.at[len(locals_)])
        locals_.append(copy)
        copy.start()
        return copy

    my_half = pl.multiple_of(core * half, half)
    other_half = pl.multiple_of((1 - core) * half, half)
    my_quarter = pl.multiple_of(my_half + y * quarter, quarter)
    other_quarter = pl.multiple_of(other_half + y * quarter, quarter)

    parity = lax.rem(y, 2)

    def piece(q, mine=True):
        side = parity if mine else 1 - parity
        return pl.ds(pl.multiple_of(side * (rows // 2) + q * chunk, chunk), chunk)

    ax = {}
    for q in range(4):
        ax[1, q] = remote(u_in.at[piece(q)], ug.at[1, 0, piece(q)], dev_x(1))
        ax[2, q] = remote(u_in.at[piece(q)], ug.at[2, 0, piece(q)], dev_x(-1))
    own_pair = remote(u_in, ug.at[0, 1], partner)
    meta_copies = []
    for slot, dx in ((0, 0), (1, 1), (2, -1), (3, 2)):
        for lane in range(2):
            if (slot, lane) == (0, 0):
                meta_copies.append(local(meta_in, meta.at[0]))
            else:
                meta_copies.append(remote(meta_in, meta.at[slot * 2 + lane], dev_x(dx, lane == 1)))
    loads = {}
    for e in range(2):
        loads[e] = (local(w_gate.at[e], w1.at[e]), local(w_up.at[e], v1.at[e]))
    w2_copies = [local(w_down.at[e, :, pl.ds(my_half, half)], w2.at[e]) for e in range(2)]
    w2_copies += [remote(w_down.at[e, :, pl.ds(other_half, half)], w2.at[2 + e], partner) for e in range(2)]
    res_copies = [local(resid.at[:, pl.ds(my_quarter, quarter)], xres.at[0]),
                  remote(resid.at[:, pl.ds(other_quarter, quarter)], xres.at[1], partner)]

    ay, pushed = {}, {1: [], 2: [], 3: []}

    def push(slot, q, mine):
        at = piece(q, mine)
        pushed[slot].append(remote(ug.at[slot, 0, at], ug.at[slot, 1, at], partner))

    def y_forward(slot, q):
        up = (q % 2 == 0) == (slot != 2)
        ay[slot, q] = remote(ug.at[slot, 0, piece(q)], ug.at[slot, 0, piece(q)], dev_y(1 if up else -1))

    def on_near(q):
        for slot in (1, 2):
            ax[slot, q].wait_recv()
            if (q % 2 == 0) == (slot == 1):
                ax[3, q] = remote(ug.at[slot, 0, piece(q)], ug.at[3, 0, piece(q)], dev_x(1 if slot == 1 else -1))
            y_forward(slot, q)
        for slot in (1, 2):
            push(slot, q, True)

    def on_far(q):
        ax[3, q].wait_recv()
        y_forward(3, q)
        push(3, q, True)

    def on_side(slot, q):
        ay[slot, q].wait_recv()
        push(slot, q, False)

    def slot_onehot(pos_row):
        return lax.broadcasted_iota(jnp.int32, (capacity, rows), 0).astype(F32) == pos_row

    def gather(slot):
        picks = []
        for lane in range(2):
            parts = []
            for e in range(2):
                pos_row = meta[slot * 2 + lane, pl.ds(2 * ep + e, 1), :]
                parts.append(slot_onehot(pos_row).astype(F32).astype(BF16))
            picks.append(jnp.concatenate(parts, axis=0))
            gates = []
            for e in range(4):
                row = 2 * (ep if e < 2 else ep_at(0, True)) + e % 2
                pos_row = meta[slot * 2 + lane, pl.ds(row, 1), :]
                gate_row = meta[slot * 2 + lane, pl.ds(experts + row, 1), :]
                gates.append(jnp.where(slot_onehot(pos_row), gate_row, 0.0))
            gate_mat = jnp.concatenate(gates, axis=0).T
            for term in range(3):
                part = gate_mat.astype(BF16)
                gsplit[lane, term] = part
                gate_mat = gate_mat - part.astype(F32)

        tiles = d_model // tile

        def fetch(t, lane):
            cols = pl.ds(pl.multiple_of(t * tile, tile), tile)
            src = u_in.at[:, cols] if (slot, lane) == (0, 0) else ug.at[slot, lane, :, cols]
            at = lax.rem(t, 2) * 2 + lane
            return pltpu.make_async_copy(src, utile.at[at], tile_sem.at[at])

        for lane in range(2):
            fetch(0, lane).start()

        def body(t, carry):
            @pl.when(t + 1 < tiles)
            def _():
                for lane in range(2):
                    fetch(t + 1, lane).start()
            cols = pl.ds(pl.multiple_of(t * tile, tile), tile)
            for lane in range(2):
                fetch(t, lane).wait()
                got = jnp.dot(picks[lane], utile[lax.rem(t, 2) * 2 + lane], preferred_element_type=F32).astype(BF16)
                for e in range(2):
                    xg[e, lane * capacity:(lane + 1) * capacity, cols] = got[e * capacity:(e + 1) * capacity]
            return carry

        lax.fori_loop(0, tiles, body, 0)

    ftile = min(256, width)

    def gate_up(e):
        def body(t, carry):
            cols = pl.ds(pl.multiple_of(t * ftile, ftile), ftile)
            gate_act = jnp.dot(xg[e], w1[e, :, cols], preferred_element_type=F32)
            up_act = jnp.dot(xg[e], v1[e, :, cols], preferred_element_type=F32)
            hid[e, :, cols] = (jax.nn.silu(gate_act) * up_act).astype(BF16)
            return carry

        lax.fori_loop(0, width // ftile, body, 0)

    dtile = min(512, half)

    def share_hidden(slot):
        return remote(hid, hpart.at[slot], partner)

    def down(slot):
        def body(t, carry):
            cols = pl.ds(pl.multiple_of(t * dtile, dtile), dtile)
            outs = []
            for e in range(4):
                lhs = hid[e] if e < 2 else hpart[slot, e - 2]
                outs.append(jnp.dot(lhs, w2[e, :, cols], preferred_element_type=F32).astype(BF16))
            for lane in range(2):
                stack = []
                for e in range(4):
                    at = lane if e < 2 else 1 - lane
                    stack.append(outs[e][at * capacity:(at + 1) * capacity])
                stacked = jnp.concatenate(stack, axis=0)
                total = jnp.dot(gsplit[lane, 0], stacked, preferred_element_type=F32)
                for term in (1, 2):
                    total += jnp.dot(gsplit[lane, term], stacked, preferred_element_type=F32)
                sums[slot, lane, :, cols] = total.astype(BF16)
            return carry

        lax.fori_loop(0, half // dtile, body, 0)

    for copy in meta_copies:
        copy.wait_recv() if copy.is_remote else copy.wait()
    own_pair.wait_recv()
    gather(0)
    for copy in loads[0]:
        copy.wait()
    gate_up(0)
    on_near(0)
    for copy in loads[1]:
        copy.wait()
    gate_up(1)
    hs = share_hidden(0)
    on_near(1)
    for copy in w2_copies:
        copy.wait_recv() if copy.is_remote else copy.wait()
    hs.wait_recv()
    down(0)
    finish_send(hs)
    on_near(2)
    for q in (0, 1):
        on_side(1, q)
        on_side(2, q)
    on_near(3)
    for q in (2,):
        on_side(1, q)
        on_side(2, q)
    on_far(0)
    on_far(1)
    for q in (3,):
        on_side(1, q)
        on_side(2, q)

    def chip_pair(slot, between):
        for copy in pushed[slot]:
            copy.wait_recv()
        gather(slot)
        gate_up(0)
        between(0)
        gate_up(1)
        between(1)
        hs = share_hidden(slot)
        between(2)
        hs.wait_recv()
        down(slot)
        finish_send(hs)

    def sub_rows(j):
        return pl.ds(j * sub, sub)

    sx = {}

    def send_sum(name, slot, lane, j, landing, dx):
        sx[name, j] = remote(sums.at[slot, lane, sub_rows(j)], landing.at[lane, sub_rows(j)], dev_x(dx))

    def during_left(step):
        if step < 2:
            on_far(2 + step)

    def during_right(step):
        for q in ((0, 1), (2,), (3,))[step]:
            on_side(3, q)

    chip_pair(1, during_left)
    for j in range(SUBS):
        send_sum('m0', 1, 0, j, rminus, -1)
    chip_pair(2, during_right)
    for j in range(SUBS):
        send_sum('p1', 2, 1, j, rplus, 1)
    chip_pair(3, lambda step: None)

    def send_far(j):
        send_sum('f0', 3, 0, j, rfar, 1)
        send_sum('f1', 3, 1, j, rfar, -1)

    def q_cols(dy):
        return pl.ds(pl.multiple_of(lax.rem(y + dy + ny, ny) * quarter, quarter), quarter)

    def stage_far(j):
        sx['f0', j].wait_recv()
        sx['f1', j].wait_recv()
        at = sub_rows(j)
        sums[2, 0, at, :] = (sums[2, 0, at, :].astype(F32) + rfar[0, at, :].astype(F32)).astype(BF16)
        send_sum('p0', 2, 0, j, rplus, 1)
        sums[1, 1, at, :] = (sums[1, 1, at, :].astype(F32) + rfar[1, at, :].astype(F32)).astype(BF16)
        send_sum('m1', 1, 1, j, rminus, -1)
        if j + 2 < SUBS:
            send_far(j + 2)

    def send_y(name, lane, j, dcol, landing, dy):
        sx[name, j] = remote(sums.at[0, lane, sub_rows(j), q_cols(dcol)], landing.at[lane, sub_rows(j)], dev_y(dy))

    def stage_own(j):
        for name in ('m0', 'p1', 'p0', 'm1'):
            sx[name, j].wait_recv()
        at = sub_rows(j)
        for lane in range(2):
            cols = q_cols(0)
            yown[lane, at, :] = sums[0, lane, at, cols].astype(F32) + rplus[lane, at, cols].astype(F32) + rminus[lane, at, cols].astype(F32)
        for lane in range(2):
            sums[0, lane, at, :] = (sums[0, lane, at, :].astype(F32) + rplus[lane, at, :].astype(F32) + rminus[lane, at, :].astype(F32)).astype(BF16)
        send_y('yf0', 0, j, 2, yfar, 1)
        send_y('yf1', 1, j, 2, yfar, -1)
        send_y('yp1', 1, j, 1, yplus, 1)
        send_y('ym0', 0, j, -1, yminus, -1)

    def stage_yfar(j):
        sx['yf0', j].wait_recv()
        sx['yf1', j].wait_recv()
        at = sub_rows(j)
        cols = q_cols(1)
        sums[0, 0, at, cols] = (sums[0, 0, at, cols].astype(F32) + yfar[0, at, :].astype(F32)).astype(BF16)
        send_y('yp0', 0, j, 1, yplus, 1)
        cols = q_cols(-1)
        sums[0, 1, at, cols] = (sums[0, 1, at, cols].astype(F32) + yfar[1, at, :].astype(F32)).astype(BF16)
        send_y('ym1', 1, j, -1, yminus, -1)

    done = {}

    def stage_final(j):
        for name in ('ym0', 'yp1', 'yp0', 'ym1'):
            sx[name, j].wait_recv()
        at = sub_rows(j)
        for lane in range(2):
            total = yown[lane, at, :] + yplus[lane, at, :].astype(F32) + yminus[lane, at, :].astype(F32)
            fin[lane, at, :] = (xres[lane, at, :].astype(F32) + total).astype(BF16)
        place = out.at[at, pl.ds(my_quarter, quarter)]
        for lane in range(2):
            done['up', lane, j] = remote(fin.at[lane, at], place, dev_y(1, lane == 1))
            done['down', lane, j] = remote(fin.at[lane, at], place, dev_y(-1, lane == 1))
        done['own', j] = local(fin.at[0, at], place)
        done['pair', j] = remote(fin.at[1, at], place, partner)

    def stage_relay(j):
        at = sub_rows(j)
        done['up', 0, j].wait_recv()
        cols = pl.ds(pl.multiple_of(my_half + lax.rem(y - 1 + ny, ny) * quarter, quarter), quarter)
        done['up2', j] = remote(out.at[at, cols], out.at[at, cols], dev_y(1))
        done['down', 1, j].wait_recv()
        cols = pl.ds(pl.multiple_of(other_half + lax.rem(y + 1, ny) * quarter, quarter), quarter)
        done['down2', j] = remote(out.at[at, cols], out.at[at, cols], dev_y(-1))

    for copy in res_copies:
        copy.wait_recv() if copy.is_remote else copy.wait()
    send_far(0)
    send_far(1)
    stages = (stage_far, stage_own, stage_yfar, stage_final, stage_relay)
    for step in range(SUBS + len(stages) - 1):
        for lag, stage in enumerate(stages):
            if 0 <= step - lag < SUBS:
                stage(step - lag)
    for j in range(SUBS):
        done['up', 1, j].wait_recv()
        done['down', 0, j].wait_recv()
        done['pair', j].wait_recv()
        done['up2', j].wait_recv()
        done['down2', j].wait_recv()
        done['own', j].wait()
    for copy in copies:
        if not any(copy is other for other in sent):
            copy.wait_send()


def solution(mesh):
    row_spec = P(('dp', 'ep'), None)
    ny, nx = mesh.shape['tp'], mesh.shape['ep'] // 2

    def device_step(resid_in, norm_scale, w_router, w_gate, w_up, w_down, choice):
        rows, d_model = resid_in.shape
        experts = w_router.shape[1]
        width = w_gate.shape[2]
        capacity = (2 * rows * choice.shape[1] + experts - 1) // experts
        normed, gate_by_expert, is_chosen = norm_route(resid_in, norm_scale, w_router, choice)
        meta = slot_meta(gate_by_expert, is_chosen, capacity)
        half, slots = d_model // 2, 2 * capacity
        quarter = half // ny
        tile = min(512, d_model)

        hbm = pl.BlockSpec(memory_space=pl.ANY)
        out, _ = pl.pallas_call(
            functools.partial(moe_kernel, experts, capacity, ny, nx),
            out_shape=(jax.ShapeDtypeStruct((rows, d_model), BF16), jax.ShapeDtypeStruct((4, 2, rows, d_model), BF16)),
            in_specs=[hbm] * 6,
            out_specs=(hbm, hbm),
            scratch_shapes=[
                pltpu.VMEM((2, d_model, width), BF16),
                pltpu.VMEM((2, d_model, width), BF16),
                pltpu.VMEM((4, width, half), BF16),
                pltpu.VMEM((2, slots, d_model), BF16),
                pltpu.VMEM((2, slots, width), BF16),
                pltpu.VMEM((4, 2, slots, width), BF16),
                pltpu.VMEM((4, 2, rows, half), BF16),
                pltpu.VMEM((2, rows, half), BF16),
                pltpu.VMEM((2, rows, half), BF16),
                pltpu.VMEM((2, rows, half), BF16),
                pltpu.VMEM((2, rows, quarter), F32),
                pltpu.VMEM((2, rows, quarter), BF16),
                pltpu.VMEM((2, rows, quarter), BF16),
                pltpu.VMEM((2, rows, quarter), BF16),
                pltpu.VMEM((2, rows, quarter), BF16),
                pltpu.VMEM((2, rows, quarter), BF16),
                pltpu.VMEM((4, rows, tile), BF16),
                pltpu.VMEM((2, 3, rows, 4 * capacity), BF16),
                pltpu.VMEM((8, 2 * experts, rows), F32),
                pltpu.SemaphoreType.DMA((16,)),
                pltpu.SemaphoreType.DMA((4,)),
                pltpu.SemaphoreType.DMA((192,)),
                pltpu.SemaphoreType.DMA((192,)),
            ],
            compiler_params=pltpu.CompilerParams(collective_id=0, has_side_effects=True, vmem_limit_bytes=67043328),
            name='moe_ring',
        )(normed, resid_in, meta, w_gate, w_up, w_down)
        return out

    return jax.shard_map(device_step, mesh=mesh, in_specs=(row_spec, P(None), P(None, None), P('ep', None, 'tp'), P('ep', None, 'tp'), P('ep', 'tp', None), row_spec), out_specs=row_spec, check_vma=False)
```

time: 444 us -> 213 us (0.48)
  Pallas kernels: 0 us -> 201 us
  waiting for transfers between devices: 181 us -> 0 us
  blocking collectives: 99.4 us -> 0 us
  local copies, waits for them, and re-layouts: 73.6 us -> 4.46 us
  matrix products: 34.4 us -> 0.83 us
  other arithmetic: 35 us -> 6.06 us
  between operations: 13.6 us -> 0.11 us
  starting transfers between devices: 6.09 us -> 0 us
    pallas_call x0 -> x1, Pallas kernels: none -> 201 us  [device_step(): pl.pallas_call(functools.partial(moe_kernel, experts, capacity, ny, nx),...]
    all_to_all x1 -> x0, blocking collectives: 99.4 us -> none  [device_step(): expert_rows = lax.all_to_all(send_rows, 'ep', 0, 1, tiled=True)]
    all_to_all x1 -> x0, waiting for transfers between devices: 92 us -> none  [device_step(): lax.all_to_all(expert_out, 'ep', 1, 0, tiled=True)]
    psum x1 -> x0, waiting for transfers between devices: 88.8 us -> none  [device_step(): tp_total = lax.psum(mixed_rows, 'tp')]
    dot_general x4 -> x2, matrix products: 34.4 us -> 0.83 us  [the longest x1 0.67 us: norm_route(): logits = jnp.dot(normed, w_router, preferred_element_type=F32)]
    gather x3 -> x0, local copies, waits for them, and re-layouts: 28.6 us -> none  [the longest x2 20.9 us: device_step(): picked_rows = jnp.take(back_rows, safe_slots, axis=0)]
    convert_element_type x1 -> x0, local copies, waits for them, and re-layouts: 22.3 us -> none  [expert_glu(): jnp.einsum('esf,efd->esd', hidden, w_down, preferred_element_type=jnp.flo...]
    all_to_all x2 -> x0, local copies, waits for them, and re-layouts: 20.3 us -> none  [the longest x1 12.6 us: device_step(): lax.all_to_all(expert_out, 'ep', 1, 0, tiled=True)]
  transfers between devices with their start and end apart: 2 -> 0, of which waited for: 2 -> 0; matrix products, arithmetic and copies ran while one was open for 0% -> 0% of each run, Pallas kernels for 0% -> 0%
where the time goes in v1:
time: 213 us; the launch traced here: 212 us
  Pallas kernels  201 us (94%)
  other arithmetic  6.06 us (3%)
  local copies, waits for them, and re-layouts  4.46 us (2%)
    pallas_call x1, Pallas kernels, device_step(): pl.pallas_call(functools.partial(moe_kernel, experts, capacity, ny, nx),...  201 us
    unnamed x11, local copies, waits for them, and re-layouts  4.46 us

profile of v1, /device:TPU:97, one launch (start us, length us, event | category | flops | bytes accessed | tf_op | source)
XLA Modules:
  0.0 212.2 jit_solution(9939041777331577755)
XLA Ops:
  0.0 0.0 copy-start
  0.0 0.0 copy-start.3
  0.0 0.0 copy-start.2
  0.0 0.0 copy-start.4
  0.0 2.1 convert_reduce_fusion
  2.1 2.3 %fusion.2 = f32[256]{0:T(256)S(1)} fusion(bf16[256,4096]{1,0:T(8,128)(2,1)} %resid.1, f32[256]{0:T(256)S(1)} %broadcast_multiply_fusion), kind=kLoop, calls=%fused_computation.4 | loop fusion | flops 4194048 | bytes 2099200 | tf_op jit(solution)/shard_map/reduce_sum | solution.py:20
  4.4 0.0 copy-done.3
  4.4 0.0 copy-done.4
  4.5 0.0 copy-done
  4.5 0.9 fusion.4.u_in
  5.4 0.0 copy-start.1
  5.4 1.3 copy-done.1
  6.7 0.0 copy-done.2
  6.7 0.7 fusion.10
  7.5 0.2 fusion.9
  7.7 0.6 pad_maximum_fusion.meta_in
  8.3 200.8 %moe_ring.1 = (bf16[256,4096]{1,0:T(8,128)(2,1)}, bf16[4,2,256,4096]{3,2,1,0:T(8,128)(2,1)}) custom-call(bf16[256,4096]{1,0:T(8,128)(2,1)} %copy-done.1, bf16[256,4096]{1,0:T(8,128)(2,1)} %resid.1, f32[32,256]{1,0:T(8,128)} %pad_maximum_fusion.meta_in, bf16[2,4096,768]{2,1,0:T(8,128)(2,1)} %w_gate.1, bf16[2,4096,768]{2,1,0:T(8,128)(2,1)} %w_up.1, ...), custom_call_target="tpu_custom_call" | custom-call | tf_op jit(solution)/shard_map/moe_ring/pallas_call | solution.py:420
  209.1 3.1 %copy.11 = bf16[256,4096]{1,0:T(8,128)(2,1)} copy(bf16[256,4096]{1,0:T(8,128)(2,1)} %get-tuple-element.6) | data formatting | bytes 4194304
  (9 shorter events, 0.1 us)
Async XLA Ops:
  0.0 4.5 %copy-start = (bf16[256,4096]{1,0:T(8,128)(2,1)S(1)}, bf16[256,4096]{1,0:T(8,128)(2,1)}, u32[]{:S(2)}) copy-start(bf16[256,4096]{1,0:T(8,128)(2,1)} %resid.1) | copy-start | bytes 6291460
  0.0 4.4 %copy-start.3 = (s32[256,2]{0,1:T(2,128)S(1)}, s32[256,2]{0,1:T(2,128)}, u32[]{:S(2)}) copy-start(s32[256,2]{0,1:T(2,128)} %param.13) | copy-start | bytes 6148
  0.0 6.7 %copy-start.2 = (bf16[4096,16]{0,1:T(8,128)(2,1)S(1)}, bf16[4096,16]{0,1:T(8,128)(2,1)}, u32[]{:S(2)}) copy-start(bf16[4096,16]{0,1:T(8,128)(2,1)} %param.9) | copy-start | bytes 393220
  0.0 4.4 %copy-start.4 = (bf16[4096]{0:T(1024)(128)(2,1)S(1)}, bf16[4096]{0:T(1024)(128)(2,1)}, u32[]{:S(2)}) copy-start(bf16[4096]{0:T(1024)(128)(2,1)} %param.8) | copy-start | bytes 24580
  5.4 1.3 copy-start.1

commit v2 on v1

--- a/solution.py
+++ b/solution.py
@@ -38,7 +38,7 @@
 
 
 def moe_kernel(experts, capacity, ny, nx, u_in, resid, meta_in, w_gate, w_up, w_down, out, ug,
-               w1, v1, w2, xg, hid, hpart, sums, rfar, rplus, rminus, yown, yfar, yplus, yminus, fin, xres, utile, gsplit, meta,
+               w1, v1, w2, xg, hid, hpart, sums, rfar, rplus, rminus, yown, yfar, yplus, yminus, ycon, vfar, vplus, vminus, wsum, wown, wfar, wplus, wminus, fin, xres, utile, gsplit, meta,
                load_sem, tile_sem, send_sem, recv_sem):
     rows, d_model = resid.shape
     half = d_model // 2
@@ -104,18 +104,18 @@
         side = parity if mine else 1 - parity
         return pl.ds(pl.multiple_of(side * (rows // 2) + q * chunk, chunk), chunk)
 
+    meta_copies = {}
+    for slot, dx in ((0, 0), (1, 1), (2, -1), (3, 2)):
+        for lane in range(2):
+            if (slot, lane) == (0, 0):
+                meta_copies[slot, lane] = local(meta_in, meta.at[0])
+            else:
+                meta_copies[slot, lane] = remote(meta_in, meta.at[slot * 2 + lane], dev_x(dx, lane == 1))
     ax = {}
     for q in range(4):
         ax[1, q] = remote(u_in.at[piece(q)], ug.at[1, 0, piece(q)], dev_x(1))
         ax[2, q] = remote(u_in.at[piece(q)], ug.at[2, 0, piece(q)], dev_x(-1))
     own_pair = remote(u_in, ug.at[0, 1], partner)
-    meta_copies = []
-    for slot, dx in ((0, 0), (1, 1), (2, -1), (3, 2)):
-        for lane in range(2):
-            if (slot, lane) == (0, 0):
-                meta_copies.append(local(meta_in, meta.at[0]))
-            else:
-                meta_copies.append(remote(meta_in, meta.at[slot * 2 + lane], dev_x(dx, lane == 1)))
     loads = {}
     for e in range(2):
         loads[e] = (local(w_gate.at[e], w1.at[e]), local(w_up.at[e], v1.at[e]))
@@ -156,6 +156,9 @@
         return lax.broadcasted_iota(jnp.int32, (capacity, rows), 0).astype(F32) == pos_row
 
     def gather(slot):
+        for lane in range(2):
+            copy = meta_copies[slot, lane]
+            copy.wait_recv() if copy.is_remote else copy.wait()
         picks = []
         for lane in range(2):
             parts = []
@@ -213,14 +216,15 @@
 
         lax.fori_loop(0, width // ftile, body, 0)
 
-    dtile = min(512, half)
+    xcols = yfar.shape[2]
+    ycols = quarter - xcols
 
     def share_hidden(slot):
         return remote(hid, hpart.at[slot], partner)
 
     def down(slot):
         def body(t, carry):
-            cols = pl.ds(pl.multiple_of(t * dtile, dtile), dtile)
+            cols = pl.ds(pl.multiple_of(t * quarter, quarter), quarter)
             outs = []
             for e in range(4):
                 lhs = hid[e] if e < 2 else hpart[slot, e - 2]
@@ -234,13 +238,67 @@
                 total = jnp.dot(gsplit[lane, 0], stacked, preferred_element_type=F32)
                 for term in (1, 2):
                     total += jnp.dot(gsplit[lane, term], stacked, preferred_element_type=F32)
-                sums[slot, lane, :, cols] = total.astype(BF16)
+                total = total.astype(BF16)
+                sums[slot, lane, :, pl.ds(pl.multiple_of(t * xcols, 128), xcols)] = total[:, :xcols]
+                ycon[slot, lane, :, pl.ds(pl.multiple_of(t * ycols, 128), ycols)] = total[:, xcols:]
             return carry
 
-        lax.fori_loop(0, half // dtile, body, 0)
-
-    for copy in meta_copies:
-        copy.wait_recv() if copy.is_remote else copy.wait()
+        lax.fori_loop(0, ny, body, 0)
+
+    rs = {}
+
+    def add_into(ref, other):
+        ref[...] = (ref[...].astype(F32) + other[...].astype(F32)).astype(BF16)
+
+    def rs_start(tag, src, landing, dev):
+        far, plus, minus = landing
+        rs[tag] = {'f0': remote(src(2, 0), far.at[0], dev(1)), 'f1': remote(src(2, 1), far.at[1], dev(-1)),
+                   'p1': remote(src(1, 1), plus.at[1], dev(1)), 'm0': remote(src(-1, 0), minus.at[0], dev(-1))}
+
+    def rs_mid(tag, src, landing, dev):
+        far, plus, minus = landing
+        rs[tag]['f0'].wait_recv()
+        add_into(src(1, 0), far.at[0])
+        rs[tag]['p0'] = remote(src(1, 0), plus.at[0], dev(1))
+        rs[tag]['f1'].wait_recv()
+        add_into(src(-1, 1), far.at[1])
+        rs[tag]['m1'] = remote(src(-1, 1), minus.at[1], dev(-1))
+
+    def rs_end(tag):
+        for name in ('m0', 'p1', 'p0', 'm1'):
+            rs[tag][name].wait_recv()
+
+    def y_args(slot):
+        def src(dy, lane):
+            return ycon.at[slot, lane, :, pl.ds(pl.multiple_of(lax.rem(y + dy + ny, ny) * ycols, 128), ycols)]
+        return src, (vfar.at[slot], vplus.at[slot], vminus.at[slot]), dev_y
+
+    def y_start(slot):
+        rs_start(slot, *y_args(slot))
+
+    def y_mid(slot):
+        rs_mid(slot, *y_args(slot))
+
+    def y_end(slot):
+        rs_end(slot)
+        src = y_args(slot)[0]
+        for lane in range(2):
+            total = src(0, lane)[...].astype(F32) + vplus[slot, lane].astype(F32) + vminus[slot, lane].astype(F32)
+            if slot == 0:
+                wown[lane] = total
+            else:
+                wsum[slot - 1, lane] = total.astype(BF16)
+
+    def w_src(dx, lane):
+        return wsum.at[{-1: 0, 1: 1, 2: 2}[dx], lane]
+
+    w_args = (w_src, (wfar, wplus, wminus), dev_x)
+
+    def w_end():
+        rs_end('w')
+        for lane in range(2):
+            wown[lane] += wplus[lane].astype(F32) + wminus[lane].astype(F32)
+
     own_pair.wait_recv()
     gather(0)
     for copy in loads[0]:
@@ -296,25 +354,41 @@
     def during_left(step):
         if step < 2:
             on_far(2 + step)
+        else:
+            y_start(0)
 
     def during_right(step):
         for q in ((0, 1), (2,), (3,))[step]:
             on_side(3, q)
+        if step == 1:
+            y_mid(0)
+            y_mid(1)
+
+    def during_far(step):
+        if step == 0:
+            y_end(0)
+            y_end(1)
+        if step == 1:
+            y_mid(2)
+        if step == 2:
+            y_end(2)
 
     chip_pair(1, during_left)
     for j in range(SUBS):
         send_sum('m0', 1, 0, j, rminus, -1)
+    y_start(1)
     chip_pair(2, during_right)
     for j in range(SUBS):
         send_sum('p1', 2, 1, j, rplus, 1)
-    chip_pair(3, lambda step: None)
+    y_start(2)
+    chip_pair(3, during_far)
 
     def send_far(j):
         send_sum('f0', 3, 0, j, rfar, 1)
         send_sum('f1', 3, 1, j, rfar, -1)
 
     def q_cols(dy):
-        return pl.ds(pl.multiple_of(lax.rem(y + dy + ny, ny) * quarter, quarter), quarter)
+        return pl.ds(pl.multiple_of(lax.rem(y + dy + ny, ny) * xcols, 128), xcols)
 
     def stage_far(j):
         sx['f0', j].wait_recv()
@@ -363,7 +437,8 @@
         at = sub_rows(j)
         for lane in range(2):
             total = yown[lane, at, :] + yplus[lane, at, :].astype(F32) + yminus[lane, at, :].astype(F32)
-            fin[lane, at, :] = (xres[lane, at, :].astype(F32) + total).astype(BF16)
+            fin[lane, at, :xcols] = (xres[lane, at, :xcols].astype(F32) + total).astype(BF16)
+            fin[lane, at, xcols:] = (xres[lane, at, xcols:].astype(F32) + wown[lane, at, :]).astype(BF16)
         place = out.at[at, pl.ds(my_quarter, quarter)]
         for lane in range(2):
             done['up', lane, j] = remote(fin.at[lane, at], place, dev_y(1, lane == 1))
@@ -384,11 +459,21 @@
         copy.wait_recv() if copy.is_remote else copy.wait()
     send_far(0)
     send_far(1)
+    y_start(3)
     stages = (stage_far, stage_own, stage_yfar, stage_final, stage_relay)
     for step in range(SUBS + len(stages) - 1):
+        if step == 3:
+            w_end()
         for lag, stage in enumerate(stages):
             if 0 <= step - lag < SUBS:
                 stage(step - lag)
+        if step == 0:
+            y_mid(3)
+        if step == 1:
+            y_end(3)
+            rs_start('w', *w_args)
+        if step == 2:
+            rs_mid('w', *w_args)
     for j in range(SUBS):
         done['up', 1, j].wait_recv()
         done['down', 0, j].wait_recv()
@@ -415,6 +500,8 @@
         half, slots = d_model // 2, 2 * capacity
         quarter = half // ny
         tile = min(512, d_model)
+        ycols = 128
+        xcols = quarter - ycols
 
         hbm = pl.BlockSpec(memory_space=pl.ANY)
         out, _ = pl.pallas_call(
@@ -429,14 +516,23 @@
                 pltpu.VMEM((2, slots, d_model), BF16),
                 pltpu.VMEM((2, slots, width), BF16),
                 pltpu.VMEM((4, 2, slots, width), BF16),
-                pltpu.VMEM((4, 2, rows, half), BF16),
-                pltpu.VMEM((2, rows, half), BF16),
-                pltpu.VMEM((2, rows, half), BF16),
-                pltpu.VMEM((2, rows, half), BF16),
-                pltpu.VMEM((2, rows, quarter), F32),
-                pltpu.VMEM((2, rows, quarter), BF16),
-                pltpu.VMEM((2, rows, quarter), BF16),
-                pltpu.VMEM((2, rows, quarter), BF16),
+                pltpu.VMEM((4, 2, rows, ny * xcols), BF16),
+                pltpu.VMEM((2, rows, ny * xcols), BF16),
+                pltpu.VMEM((2, rows, ny * xcols), BF16),
+                pltpu.VMEM((2, rows, ny * xcols), BF16),
+                pltpu.VMEM((2, rows, xcols), F32),
+                pltpu.VMEM((2, rows, xcols), BF16),
+                pltpu.VMEM((2, rows, xcols), BF16),
+                pltpu.VMEM((2, rows, xcols), BF16),
+                pltpu.VMEM((4, 2, rows, ny * ycols), BF16),
+                pltpu.VMEM((4, 2, rows, ycols), BF16),
+                pltpu.VMEM((4, 2, rows, ycols), BF16),
+                pltpu.VMEM((4, 2, rows, ycols), BF16),
+                pltpu.VMEM((3, 2, rows, ycols), BF16),
+                pltpu.VMEM((2, rows, ycols), F32),
+                pltpu.VMEM((2, rows, ycols), BF16),
+                pltpu.VMEM((2, rows, ycols), BF16),
+                pltpu.VMEM((2, rows, ycols), BF16),
                 pltpu.VMEM((2, rows, quarter), BF16),
                 pltpu.VMEM((2, rows, quarter), BF16),
                 pltpu.VMEM((4, rows, tile), BF16),
@@ -444,8 +540,8 @@
                 pltpu.VMEM((8, 2 * experts, rows), F32),
                 pltpu.SemaphoreType.DMA((16,)),
                 pltpu.SemaphoreType.DMA((4,)),
-                pltpu.SemaphoreType.DMA((192,)),
-                pltpu.SemaphoreType.DMA((192,)),
+                pltpu.SemaphoreType.DMA((256,)),
+                pltpu.SemaphoreType.DMA((256,)),
             ],
             compiler_params=pltpu.CompilerParams(collective_id=0, has_side_effects=True, vmem_limit_bytes=67043328),
             name='moe_ring',

time: 213 us -> 184 us (0.86)
  Pallas kernels: 201 us -> 172 us
    pallas_call x1, Pallas kernels: 201 us -> 172 us  [device_step(): pl.pallas_call(functools.partial(moe_kernel, experts, capacity, ny, nx),...]
where the time goes in v2:
time: 184 us
  Pallas kernels  172 us (93%)
  other arithmetic  6.06 us (3%)
  local copies, waits for them, and re-layouts  4.46 us (2%)
    pallas_call x1, Pallas kernels, device_step(): pl.pallas_call(functools.partial(moe_kernel, experts, capacity, ny, nx),...  172 us
    unnamed x11, local copies, waits for them, and re-layouts  4.46 us

profile of v2, /device:TPU:97, one launch (start us, length us, event | category | flops | bytes accessed | tf_op | source)
XLA Modules:
  0.0 183.7 jit_solution(3666985283469981708)
XLA Ops:
  0.0 0.0 copy-start
  0.0 0.0 copy-start.3
  0.0 0.0 copy-start.2
  0.0 0.0 copy-start.4
  0.0 2.1 %convert_reduce_fusion = f32[256]{0:T(256)S(1)} fusion(bf16[256,4096]{1,0:T(8,128)(2,1)} %resid.1), kind=kLoop, calls=%fused_computation.1 | loop fusion | flops 2096896 | bytes 2098176 | tf_op jit(solution)/shard_map/reduce_sum | solution.py:19
  2.1 2.3 %fusion.2 = f32[256]{0:T(256)S(1)} fusion(bf16[256,4096]{1,0:T(8,128)(2,1)} %resid.1, f32[256]{0:T(256)S(1)} %broadcast_multiply_fusion), kind=kLoop, calls=%fused_computation.4 | loop fusion | flops 4194048 | bytes 2099200 | tf_op jit(solution)/shard_map/reduce_sum | solution.py:20
  4.4 0.0 copy-done.3
  4.4 0.0 copy-done.4
  4.5 0.0 copy-done
  4.5 0.9 fusion.4.u_in
  5.4 0.0 copy-start.1
  5.4 1.3 copy-done.1
  6.7 0.0 copy-done.2
  6.7 0.7 fusion.10
  7.5 0.2 fusion.9
  7.7 0.6 pad_maximum_fusion.meta_in
  8.3 172.2 %moe_ring.1 = (bf16[256,4096]{1,0:T(8,128)(2,1)}, bf16[4,2,256,4096]{3,2,1,0:T(8,128)(2,1)}) custom-call(bf16[256,4096]{1,0:T(8,128)(2,1)} %copy-done.1, bf16[256,4096]{1,0:T(8,128)(2,1)} %resid.1, f32[32,256]{1,0:T(8,128)} %pad_maximum_fusion.meta_in, bf16[2,4096,768]{2,1,0:T(8,128)(2,1)} %w_gate.1, bf16[2,4096,768]{2,1,0:T(8,128)(2,1)} %w_up.1, ...), custom_call_target="tpu_custom_call" | custom-call | tf_op jit(solution)/shard_map/moe_ring/pallas_call | solution.py:507
  180.6 3.1 %copy.11 = bf16[256,4096]{1,0:T(8,128)(2,1)} copy(bf16[256,4096]{1,0:T(8,128)(2,1)} %get-tuple-element.6) | data formatting | bytes 4194304
  (9 shorter events, 0.1 us)
Async XLA Ops:
  0.0 4.5 %copy-start = (bf16[256,4096]{1,0:T(8,128)(2,1)S(1)}, bf16[256,4096]{1,0:T(8,128)(2,1)}, u32[]{:S(2)}) copy-start(bf16[256,4096]{1,0:T(8,128)(2,1)} %resid.1) | copy-start | bytes 6291460
  0.0 4.4 %copy-start.3 = (s32[256,2]{0,1:T(2,128)S(1)}, s32[256,2]{0,1:T(2,128)}, u32[]{:S(2)}) copy-start(s32[256,2]{0,1:T(2,128)} %param.13) | copy-start | bytes 6148
  0.0 6.7 %copy-start.2 = (bf16[4096,16]{0,1:T(8,128)(2,1)S(1)}, bf16[4096,16]{0,1:T(8,128)(2,1)}, u32[]{:S(2)}) copy-start(bf16[4096,16]{0,1:T(8,128)(2,1)} %param.9) | copy-start | bytes 393220
  0.0 4.4 %copy-start.4 = (bf16[4096]{0:T(1024)(128)(2,1)S(1)}, bf16[4096]{0:T(1024)(128)(2,1)}, u32[]{:S(2)}) copy-start(bf16[4096]{0:T(1024)(128)(2,1)} %param.8) | copy-start | bytes 24580
  5.4 1.3 copy-start.1

commit v3 on v2

--- a/solution.py
+++ b/solution.py
@@ -46,7 +46,6 @@
     width = w_gate.shape[2]
     chunk = rows // 8
     sub = rows // SUBS
-    tile = utile.shape[2]
     y = lax.axis_index('tp')
     ep = lax.axis_index('ep')
     core = lax.rem(ep, 2)
@@ -155,6 +154,21 @@
     def slot_onehot(pos_row):
         return lax.broadcasted_iota(jnp.int32, (capacity, rows), 0).astype(F32) == pos_row
 
+    tile = min(512, d_model)
+    tiles = d_model // tile
+
+    def fetch(slot, t, lane):
+        cols = pl.ds(t * tile, tile) if isinstance(t, int) else pl.ds(pl.multiple_of(t * tile, tile), tile)
+        src = u_in.at[:, cols] if (slot, lane) == (0, 0) else ug.at[slot, lane, :, cols]
+        return pltpu.make_async_copy(src, utile.at[lane, :, cols], tile_sem.at[lane * tiles + t])
+
+    def prefetch(slot):
+        for copy in pushed.get(slot, ()):
+            copy.wait_recv()
+        for t in range(tiles):
+            for lane in range(2):
+                fetch(slot, t, lane).start()
+
     def gather(slot):
         for lane in range(2):
             copy = meta_copies[slot, lane]
@@ -178,26 +192,11 @@
                 gsplit[lane, term] = part
                 gate_mat = gate_mat - part.astype(F32)
 
-        tiles = d_model // tile
-
-        def fetch(t, lane):
-            cols = pl.ds(pl.multiple_of(t * tile, tile), tile)
-            src = u_in.at[:, cols] if (slot, lane) == (0, 0) else ug.at[slot, lane, :, cols]
-            at = lax.rem(t, 2) * 2 + lane
-            return pltpu.make_async_copy(src, utile.at[at], tile_sem.at[at])
-
-        for lane in range(2):
-            fetch(0, lane).start()
-
         def body(t, carry):
-            @pl.when(t + 1 < tiles)
-            def _():
-                for lane in range(2):
-                    fetch(t + 1, lane).start()
             cols = pl.ds(pl.multiple_of(t * tile, tile), tile)
             for lane in range(2):
-                fetch(t, lane).wait()
-                got = jnp.dot(picks[lane], utile[lax.rem(t, 2) * 2 + lane], preferred_element_type=F32).astype(BF16)
+                fetch(slot, t, lane).wait()
+                got = jnp.dot(picks[lane], utile[lane, :, cols], preferred_element_type=F32).astype(BF16)
                 for e in range(2):
                     xg[e, lane * capacity:(lane + 1) * capacity, cols] = got[e * capacity:(e + 1) * capacity]
             return carry
@@ -300,6 +299,7 @@
             wown[lane] += wplus[lane].astype(F32) + wminus[lane].astype(F32)
 
     own_pair.wait_recv()
+    prefetch(0)
     gather(0)
     for copy in loads[0]:
         copy.wait()
@@ -330,9 +330,9 @@
         on_side(2, q)
 
     def chip_pair(slot, between):
-        for copy in pushed[slot]:
-            copy.wait_recv()
         gather(slot)
+        if slot == 1:
+            prefetch(2)
         gate_up(0)
         between(0)
         gate_up(1)
@@ -363,6 +363,8 @@
         if step == 1:
             y_mid(0)
             y_mid(1)
+        if step == 2:
+            prefetch(3)
 
     def during_far(step):
         if step == 0:
@@ -373,6 +375,7 @@
         if step == 2:
             y_end(2)
 
+    prefetch(1)
     chip_pair(1, during_left)
     for j in range(SUBS):
         send_sum('m0', 1, 0, j, rminus, -1)
@@ -499,7 +502,6 @@
         meta = slot_meta(gate_by_expert, is_chosen, capacity)
         half, slots = d_model // 2, 2 * capacity
         quarter = half // ny
-        tile = min(512, d_model)
         ycols = 128
         xcols = quarter - ycols
 
@@ -535,11 +537,11 @@
                 pltpu.VMEM((2, rows, ycols), BF16),
                 pltpu.VMEM((2, rows, quarter), BF16),
                 pltpu.VMEM((2, rows, quarter), BF16),
-                pltpu.VMEM((4, rows, tile), BF16),
+                pltpu.VMEM((2, rows, d_model), BF16),
                 pltpu.VMEM((2, 3, rows, 4 * capacity), BF16),
                 pltpu.VMEM((8, 2 * experts, rows), F32),
                 pltpu.SemaphoreType.DMA((16,)),
-                pltpu.SemaphoreType.DMA((4,)),
+                pltpu.SemaphoreType.DMA((2 * (d_model // min(512, d_model)),)),
                 pltpu.SemaphoreType.DMA((256,)),
                 pltpu.SemaphoreType.DMA((256,)),
             ],

time: 184 us -> 176 us (0.957)
  Pallas kernels: 172 us -> 164 us
    pallas_call x1, Pallas kernels: 172 us -> 164 us  [device_step(): pl.pallas_call(functools.partial(moe_kernel, experts, capacity, ny, nx),...]
where the time goes in v3:
time: 176 us; the launch traced here: 175 us
  Pallas kernels  164 us (93%)
  other arithmetic  6.06 us (3%)
  local copies, waits for them, and re-layouts  4.46 us (3%)
    pallas_call x1, Pallas kernels, device_step(): pl.pallas_call(functools.partial(moe_kernel, experts, capacity, ny, nx),...  164 us
    unnamed x11, local copies, waits for them, and re-layouts  4.46 us

profile of v3, /device:TPU:97, one launch (start us, length us, event | category | flops | bytes accessed | tf_op | source)
XLA Modules:
  0.0 175.5 jit_solution(10763086891173736006)
XLA Ops:
  0.0 0.0 copy-start
  0.0 0.0 copy-start.3
  0.0 0.0 copy-start.2
  0.0 0.0 copy-start.4
  0.0 2.1 %convert_reduce_fusion = f32[256]{0:T(256)S(1)} fusion(bf16[256,4096]{1,0:T(8,128)(2,1)} %resid.1), kind=kLoop, calls=%fused_computation.1 | loop fusion | flops 2096896 | bytes 2098176 | tf_op jit(solution)/shard_map/reduce_sum | solution.py:19
  2.1 2.3 %fusion.2 = f32[256]{0:T(256)S(1)} fusion(bf16[256,4096]{1,0:T(8,128)(2,1)} %resid.1, f32[256]{0:T(256)S(1)} %broadcast_multiply_fusion), kind=kLoop, calls=%fused_computation.4 | loop fusion | flops 4194048 | bytes 2099200 | tf_op jit(solution)/shard_map/reduce_sum | solution.py:20
  4.4 0.0 copy-done.3
  4.4 0.0 copy-done.4
  4.5 0.0 copy-done
  4.5 0.9 fusion.4.u_in
  5.4 0.0 copy-start.1
  5.4 1.3 copy-done.1
  6.7 0.0 copy-done.2
  6.7 0.7 fusion.10
  7.5 0.2 fusion.9
  7.7 0.6 pad_maximum_fusion.meta_in
  8.3 164.0 %moe_ring.1 = (bf16[256,4096]{1,0:T(8,128)(2,1)}, bf16[4,2,256,4096]{3,2,1,0:T(8,128)(2,1)}) custom-call(bf16[256,4096]{1,0:T(8,128)(2,1)} %copy-done.1, bf16[256,4096]{1,0:T(8,128)(2,1)} %resid.1, f32[32,256]{1,0:T(8,128)} %pad_maximum_fusion.meta_in, bf16[2,4096,768]{2,1,0:T(8,128)(2,1)} %w_gate.1, bf16[2,4096,768]{2,1,0:T(8,128)(2,1)} %w_up.1, ...), custom_call_target="tpu_custom_call" | custom-call | tf_op jit(solution)/shard_map/moe_ring/pallas_call | solution.py:509
  172.3 3.1 %copy.11 = bf16[256,4096]{1,0:T(8,128)(2,1)} copy(bf16[256,4096]{1,0:T(8,128)(2,1)} %get-tuple-element.6) | data formatting | bytes 4194304
  (9 shorter events, 0.1 us)
Async XLA Ops:
  0.0 4.5 %copy-start = (bf16[256,4096]{1,0:T(8,128)(2,1)S(1)}, bf16[256,4096]{1,0:T(8,128)(2,1)}, u32[]{:S(2)}) copy-start(bf16[256,4096]{1,0:T(8,128)(2,1)} %resid.1) | copy-start | bytes 6291460
  0.0 4.4 %copy-start.3 = (s32[256,2]{0,1:T(2,128)S(1)}, s32[256,2]{0,1:T(2,128)}, u32[]{:S(2)}) copy-start(s32[256,2]{0,1:T(2,128)} %param.13) | copy-start | bytes 6148
  0.0 6.7 %copy-start.2 = (bf16[4096,16]{0,1:T(8,128)(2,1)S(1)}, bf16[4096,16]{0,1:T(8,128)(2,1)}, u32[]{:S(2)}) copy-start(bf16[4096,16]{0,1:T(8,128)(2,1)} %param.9) | copy-start | bytes 393220
  0.0 4.4 %copy-start.4 = (bf16[4096]{0:T(1024)(128)(2,1)S(1)}, bf16[4096]{0:T(1024)(128)(2,1)}, u32[]{:S(2)}) copy-start(bf16[4096]{0:T(1024)(128)(2,1)} %param.8) | copy-start | bytes 24580
  5.4 1.3 copy-start.1

commit v4 on v3

--- a/solution.py
+++ b/solution.py
@@ -12,6 +12,22 @@
 BF16 = jnp.bfloat16
 F32 = jnp.float32
 SUBS = 4
+PIECES = 4
+LATE_X_SHARE = 2
+ORDER = (
+    ('ns', 2, 1), ('ns', 1, 0), ('ns', 2, 3), ('ns', 1, 2), ('G', 0), ('A', 2, 1), ('A', 1, 0), ('T', 0), ('A', 1, 2),
+    ('ns', 1, 1), ('A', 2, 3), ('ns', 1, 3), ('ns', 2, 2), ('ns', 2, 0), ('U0', 0), ('U1', 0), ('A', 3, 0), ('H', 0),
+    ('A', 3, 1), ('A', 3, 2), ('S', 1, 0), ('A', 3, 3), ('D', 0), ('S', 1, 2), ('S', 3, 0), ('S', 3, 1), ('A', 1, 1),
+    ('A', 2, 2), ('meta',), ('S', 3, 2), ('S', 3, 3), ('S', 2, 3), ('PF', 3), ('A', 2, 0), ('A', 1, 3), ('G', 3),
+    ('YS', 0), ('U0', 3), ('S', 1, 1), ('U1', 3), ('H', 3), ('T', 3), ('S', 1, 3), ('S', 2, 2), ('PF', 1), ('S', 2, 1),
+    ('D', 3), ('S', 2, 0), ('YS', 3), ('f1', 3), ('f1', 1), ('G', 1), ('PF', 2), ('U0', 1), ('T', 1), ('f0', 3),
+    ('U1', 1), ('H', 1), ('f0', 1), ('G', 2), ('f0', 2), ('f1', 0), ('D', 1), ('m0', 0), ('m0', 3), ('YS', 1),
+    ('U0', 2), ('U1', 2), ('H', 2), ('f0', 0), ('m1', 1), ('YM', 3), ('m0', 1), ('T', 2), ('f1', 2), ('D', 2),
+    ('YS', 2), ('p1', 0), ('p0', 0), ('YE', 3), ('m1', 3), ('YM', 1), ('p1', 1), ('YM', 2), ('p0', 1), ('YM', 0),
+    ('m1', 0), ('p0', 3), ('p1', 3), ('wf',), ('m0', 2), ('O', 1), ('O', 0), ('p1', 2), ('YE', 1), ('wm1',), ('m1', 2),
+    ('p0', 2), ('V', 1), ('V', 0), ('O', 3), ('N', 1), ('V', 3), ('YE', 2), ('wm0',), ('YE', 0), ('wp1',), ('N', 0),
+    ('R', 1), ('wp0',), ('N', 3), ('O', 2), ('R', 0), ('R', 3), ('V', 2), ('WS',), ('N', 2), ('WR',), ('R', 2),
+)
 
 
 def norm_route(resid_rows, norm_scale, w_router, choice_rows):
@@ -29,22 +45,24 @@
     return normed, gate_by_expert, jnp.any(chosen, axis=1)
 
 
-def slot_meta(gate_by_expert, is_chosen, capacity):
+def slot_meta(gate_by_expert, is_chosen, capacity, chips):
     rows = is_chosen.shape[0]
     earlier = jnp.arange(rows)[:, None] > jnp.arange(rows)[None, :]
     position = jnp.dot(earlier.astype(BF16), is_chosen.astype(BF16), preferred_element_type=F32)
     kept = is_chosen & (position < capacity)
-    return jnp.concatenate([jnp.where(kept, position, -1.0).T, jnp.where(kept, gate_by_expert, 0.0).T], axis=0)
-
-
-def moe_kernel(experts, capacity, ny, nx, u_in, resid, meta_in, w_gate, w_up, w_down, out, ug,
+    slots = jnp.where(kept, position, -1.0).T.reshape(chips, -1, rows)
+    gates = jnp.where(kept, gate_by_expert, 0.0).T.reshape(chips, -1, rows)
+    return jnp.concatenate([slots, gates], axis=1)
+
+
+def moe_kernel(capacity, ny, nx, u_in, resid, meta_in, w_gate, w_up, w_down, out, ug,
                w1, v1, w2, xg, hid, hpart, sums, rfar, rplus, rminus, yown, yfar, yplus, yminus, ycon, vfar, vplus, vminus, wsum, wown, wfar, wplus, wminus, fin, xres, utile, gsplit, meta,
                load_sem, tile_sem, send_sem, recv_sem):
     rows, d_model = resid.shape
     half = d_model // 2
     quarter = half // ny
     width = w_gate.shape[2]
-    chunk = rows // 8
+    chunk = rows // (2 * PIECES)
     sub = rows // SUBS
     y = lax.axis_index('tp')
     ep = lax.axis_index('ep')
@@ -103,18 +121,22 @@
         side = parity if mine else 1 - parity
         return pl.ds(pl.multiple_of(side * (rows // 2) + q * chunk, chunk), chunk)
 
-    meta_copies = {}
-    for slot, dx in ((0, 0), (1, 1), (2, -1), (3, 2)):
-        for lane in range(2):
-            if (slot, lane) == (0, 0):
-                meta_copies[slot, lane] = local(meta_in, meta.at[0])
-            else:
-                meta_copies[slot, lane] = remote(meta_in, meta.at[slot * 2 + lane], dev_x(dx, lane == 1))
+    def meta_for(dx):
+        return meta_in.at[lax.rem(x + dx + nx, nx)]
+
     ax = {}
-    for q in range(4):
-        ax[1, q] = remote(u_in.at[piece(q)], ug.at[1, 0, piece(q)], dev_x(1))
-        ax[2, q] = remote(u_in.at[piece(q)], ug.at[2, 0, piece(q)], dev_x(-1))
-    own_pair = remote(u_in, ug.at[0, 1], partner)
+
+    def near_send(slot, q):
+        ax[slot, q] = remote(u_in.at[piece(q)], ug.at[slot, 0, piece(q)], dev_x(1 if slot == 1 else -1))
+
+    own_rows = (local(u_in, utile.at[0]), remote(u_in, utile.at[1], partner))
+    meta_copies = {(0, 0): local(meta_for(0), meta.at[0]), (0, 1): remote(meta_for(0), meta.at[1], partner)}
+
+    def send_meta():
+        for slot, dx in ((1, 1), (2, -1), (3, 2)):
+            for lane in range(2):
+                meta_copies[slot, lane] = remote(meta_for(dx), meta.at[slot * 2 + lane], dev_x(dx, lane == 1))
+
     loads = {}
     for e in range(2):
         loads[e] = (local(w_gate.at[e], w1.at[e]), local(w_up.at[e], v1.at[e]))
@@ -130,22 +152,15 @@
         pushed[slot].append(remote(ug.at[slot, 0, at], ug.at[slot, 1, at], partner))
 
     def y_forward(slot, q):
-        up = (q % 2 == 0) == (slot != 2)
+        up = slot == 1 or (slot == 3 and q % 2 == 0)
         ay[slot, q] = remote(ug.at[slot, 0, piece(q)], ug.at[slot, 0, piece(q)], dev_y(1 if up else -1))
 
-    def on_near(q):
-        for slot in (1, 2):
-            ax[slot, q].wait_recv()
-            if (q % 2 == 0) == (slot == 1):
-                ax[3, q] = remote(ug.at[slot, 0, piece(q)], ug.at[3, 0, piece(q)], dev_x(1 if slot == 1 else -1))
-            y_forward(slot, q)
-        for slot in (1, 2):
-            push(slot, q, True)
-
-    def on_far(q):
-        ax[3, q].wait_recv()
-        y_forward(3, q)
-        push(3, q, True)
+    def on_piece(slot, q):
+        ax[slot, q].wait_recv()
+        if slot == 2 - (q + 1) % 2:
+            ax[3, q] = remote(ug.at[slot, 0, piece(q)], ug.at[3, 0, piece(q)], dev_x(1 if slot == 1 else -1))
+        y_forward(slot, q)
+        push(slot, q, True)
 
     def on_side(slot, q):
         ay[slot, q].wait_recv()
@@ -154,48 +169,52 @@
     def slot_onehot(pos_row):
         return lax.broadcasted_iota(jnp.int32, (capacity, rows), 0).astype(F32) == pos_row
 
-    tile = min(512, d_model)
+    tile = min(1024, d_model)
     tiles = d_model // tile
 
     def fetch(slot, t, lane):
         cols = pl.ds(t * tile, tile) if isinstance(t, int) else pl.ds(pl.multiple_of(t * tile, tile), tile)
-        src = u_in.at[:, cols] if (slot, lane) == (0, 0) else ug.at[slot, lane, :, cols]
-        return pltpu.make_async_copy(src, utile.at[lane, :, cols], tile_sem.at[lane * tiles + t])
+        return pltpu.make_async_copy(ug.at[slot, lane, :, cols], utile.at[lane, :, cols], tile_sem.at[lane * tiles + t])
 
     def prefetch(slot):
-        for copy in pushed.get(slot, ()):
+        for copy in pushed[slot]:
             copy.wait_recv()
         for t in range(tiles):
             for lane in range(2):
                 fetch(slot, t, lane).start()
 
-    def gather(slot):
-        for lane in range(2):
-            copy = meta_copies[slot, lane]
-            copy.wait_recv() if copy.is_remote else copy.wait()
-        picks = []
+    def meta_rows(slot, lane, e):
+        row = 2 * core + e if e < 2 else 2 * (1 - core) + e - 2
+        return meta[slot * 2 + lane, pl.ds(row, 1), :], meta[slot * 2 + lane, pl.ds(4 + row, 1), :]
+
+    def gates(slot):
         for lane in range(2):
             parts = []
-            for e in range(2):
-                pos_row = meta[slot * 2 + lane, pl.ds(2 * ep + e, 1), :]
-                parts.append(slot_onehot(pos_row).astype(F32).astype(BF16))
-            picks.append(jnp.concatenate(parts, axis=0))
-            gates = []
             for e in range(4):
-                row = 2 * (ep if e < 2 else ep_at(0, True)) + e % 2
-                pos_row = meta[slot * 2 + lane, pl.ds(row, 1), :]
-                gate_row = meta[slot * 2 + lane, pl.ds(experts + row, 1), :]
-                gates.append(jnp.where(slot_onehot(pos_row), gate_row, 0.0))
-            gate_mat = jnp.concatenate(gates, axis=0).T
+                pos_row, gate_row = meta_rows(slot, lane, e)
+                parts.append(jnp.where(slot_onehot(pos_row), gate_row, 0.0))
+            gate_mat = jnp.concatenate(parts, axis=0).T
             for term in range(3):
                 part = gate_mat.astype(BF16)
                 gsplit[lane, term] = part
                 gate_mat = gate_mat - part.astype(F32)
 
+    def gather(slot):
+        picks = []
+        for lane in range(2):
+            copy = meta_copies[slot, lane]
+            copy.wait_recv() if copy.is_remote else copy.wait()
+            parts = [slot_onehot(meta_rows(slot, lane, e)[0]).astype(F32).astype(BF16) for e in range(2)]
+            picks.append(jnp.concatenate(parts, axis=0))
+        if slot == 0:
+            own_rows[0].wait()
+            own_rows[1].wait_recv()
+
         def body(t, carry):
             cols = pl.ds(pl.multiple_of(t * tile, tile), tile)
             for lane in range(2):
-                fetch(slot, t, lane).wait()
+                if slot:
+                    fetch(slot, t, lane).wait()
                 got = jnp.dot(picks[lane], utile[lane, :, cols], preferred_element_type=F32).astype(BF16)
                 for e in range(2):
                     xg[e, lane * capacity:(lane + 1) * capacity, cols] = got[e * capacity:(e + 1) * capacity]
@@ -205,7 +224,11 @@
 
     ftile = min(256, width)
 
-    def gate_up(e):
+    def gate_up(e, slot):
+        if slot == 0:
+            for copy in loads[e]:
+                copy.wait()
+
         def body(t, carry):
             cols = pl.ds(pl.multiple_of(t * ftile, ftile), ftile)
             gate_act = jnp.dot(xg[e], w1[e, :, cols], preferred_element_type=F32)
@@ -218,10 +241,17 @@
     xcols = yfar.shape[2]
     ycols = quarter - xcols
 
+    shared = {}
+
     def share_hidden(slot):
-        return remote(hid, hpart.at[slot], partner)
+        shared[slot] = remote(hid, hpart.at[slot], partner)
 
     def down(slot):
+        if slot == 0:
+            for copy in w2_copies:
+                copy.wait_recv() if copy.is_remote else copy.wait()
+        shared[slot].wait_recv()
+
         def body(t, carry):
             cols = pl.ds(pl.multiple_of(t * quarter, quarter), quarter)
             outs = []
@@ -243,6 +273,7 @@
             return carry
 
         lax.fori_loop(0, ny, body, 0)
+        finish_send(shared[slot])
 
     rs = {}
 
@@ -291,57 +322,19 @@
     def w_src(dx, lane):
         return wsum.at[{-1: 0, 1: 1, 2: 2}[dx], lane]
 
-    w_args = (w_src, (wfar, wplus, wminus), dev_x)
-
-    def w_end():
-        rs_end('w')
-        for lane in range(2):
-            wown[lane] += wplus[lane].astype(F32) + wminus[lane].astype(F32)
-
-    own_pair.wait_recv()
-    prefetch(0)
-    gather(0)
-    for copy in loads[0]:
-        copy.wait()
-    gate_up(0)
-    on_near(0)
-    for copy in loads[1]:
-        copy.wait()
-    gate_up(1)
-    hs = share_hidden(0)
-    on_near(1)
-    for copy in w2_copies:
-        copy.wait_recv() if copy.is_remote else copy.wait()
-    hs.wait_recv()
-    down(0)
-    finish_send(hs)
-    on_near(2)
-    for q in (0, 1):
-        on_side(1, q)
-        on_side(2, q)
-    on_near(3)
-    for q in (2,):
-        on_side(1, q)
-        on_side(2, q)
-    on_far(0)
-    on_far(1)
-    for q in (3,):
-        on_side(1, q)
-        on_side(2, q)
-
-    def chip_pair(slot, between):
-        gather(slot)
-        if slot == 1:
-            prefetch(2)
-        gate_up(0)
-        between(0)
-        gate_up(1)
-        between(1)
-        hs = share_hidden(slot)
-        between(2)
-        hs.wait_recv()
-        down(slot)
-        finish_send(hs)
+    def w_far():
+        rs['w'] = {'f0': remote(w_src(2, 0), wfar.at[0], dev_x(1)), 'f1': remote(w_src(2, 1), wfar.at[1], dev_x(-1))}
+
+    wx = {}
+
+    def w_send(name):
+        lane = int(name[1])
+        dx = 1 if name[0] == 'p' else -1
+        if name in ('p0', 'm1'):
+            rs['w']['f%d' % lane].wait_recv()
+            add_into(w_src(dx, lane), wfar.at[lane])
+        landing = wplus if dx == 1 else wminus
+        wx[name] = remote(w_src(dx, lane), landing.at[lane], dev_x(dx))
 
     def sub_rows(j):
         return pl.ds(j * sub, sub)
@@ -351,58 +344,19 @@
     def send_sum(name, slot, lane, j, landing, dx):
         sx[name, j] = remote(sums.at[slot, lane, sub_rows(j)], landing.at[lane, sub_rows(j)], dev_x(dx))
 
-    def during_left(step):
-        if step < 2:
-            on_far(2 + step)
-        else:
-            y_start(0)
-
-    def during_right(step):
-        for q in ((0, 1), (2,), (3,))[step]:
-            on_side(3, q)
-        if step == 1:
-            y_mid(0)
-            y_mid(1)
-        if step == 2:
-            prefetch(3)
-
-    def during_far(step):
-        if step == 0:
-            y_end(0)
-            y_end(1)
-        if step == 1:
-            y_mid(2)
-        if step == 2:
-            y_end(2)
-
-    prefetch(1)
-    chip_pair(1, during_left)
-    for j in range(SUBS):
-        send_sum('m0', 1, 0, j, rminus, -1)
-    y_start(1)
-    chip_pair(2, during_right)
-    for j in range(SUBS):
-        send_sum('p1', 2, 1, j, rplus, 1)
-    y_start(2)
-    chip_pair(3, during_far)
-
-    def send_far(j):
-        send_sum('f0', 3, 0, j, rfar, 1)
-        send_sum('f1', 3, 1, j, rfar, -1)
+    def x_send(name, j):
+        lane = int(name[1])
+        if name[0] == 'f':
+            send_sum(name, 3, lane, j, rfar, 1 if lane == 0 else -1)
+            return
+        slot, landing, dx = (2, rplus, 1) if name[0] == 'p' else (1, rminus, -1)
+        if name in ('p0', 'm1'):
+            sx['f%d' % lane, j].wait_recv()
+            add_into(sums.at[slot, lane, sub_rows(j)], rfar.at[lane, sub_rows(j)])
+        send_sum(name, slot, lane, j, landing, dx)
 
     def q_cols(dy):
         return pl.ds(pl.multiple_of(lax.rem(y + dy + ny, ny) * xcols, 128), xcols)
-
-    def stage_far(j):
-        sx['f0', j].wait_recv()
-        sx['f1', j].wait_recv()
-        at = sub_rows(j)
-        sums[2, 0, at, :] = (sums[2, 0, at, :].astype(F32) + rfar[0, at, :].astype(F32)).astype(BF16)
-        send_sum('p0', 2, 0, j, rplus, 1)
-        sums[1, 1, at, :] = (sums[1, 1, at, :].astype(F32) + rfar[1, at, :].astype(F32)).astype(BF16)
-        send_sum('m1', 1, 1, j, rminus, -1)
-        if j + 2 < SUBS:
-            send_far(j + 2)
 
     def send_y(name, lane, j, dcol, landing, dy):
         sx[name, j] = remote(sums.at[0, lane, sub_rows(j), q_cols(dcol)], landing.at[lane, sub_rows(j)], dev_y(dy))
@@ -433,57 +387,75 @@
         send_y('ym1', 1, j, -1, yminus, -1)
 
     done = {}
+    pending = [res_copies]
+
+    def residual_ready():
+        for copy in pending.pop() if pending else ():
+            copy.wait_recv() if copy.is_remote else copy.wait()
+
+    def share_rows(key, at, first, cols):
+        def place(start):
+            return out.at[at, pl.ds(pl.multiple_of(start + first, 128), cols)]
+
+        src = fin.at[:, at, pl.ds(first, cols)]
+        for lane in range(2):
+            done['up', lane, key] = remote(src.at[lane], place(my_quarter), dev_y(1, lane == 1))
+            done['down', lane, key] = remote(src.at[lane], place(my_quarter), dev_y(-1, lane == 1))
+        done['own', key] = local(src.at[0], place(my_quarter))
+        done['pair', key] = remote(src.at[1], place(my_quarter), partner)
+
+    def relay_rows(key, at, first, cols):
+        def place(start):
+            return out.at[at, pl.ds(pl.multiple_of(start + first, 128), cols)]
+
+        done['up', 0, key].wait_recv()
+        start = my_half + lax.rem(y - 1 + ny, ny) * quarter
+        done['up2', key] = remote(place(start), place(start), dev_y(1))
+        done['down', 1, key].wait_recv()
+        start = other_half + lax.rem(y + 1, ny) * quarter
+        done['down2', key] = remote(place(start), place(start), dev_y(-1))
 
     def stage_final(j):
         for name in ('ym0', 'yp1', 'yp0', 'ym1'):
             sx[name, j].wait_recv()
+        residual_ready()
         at = sub_rows(j)
         for lane in range(2):
             total = yown[lane, at, :] + yplus[lane, at, :].astype(F32) + yminus[lane, at, :].astype(F32)
             fin[lane, at, :xcols] = (xres[lane, at, :xcols].astype(F32) + total).astype(BF16)
-            fin[lane, at, xcols:] = (xres[lane, at, xcols:].astype(F32) + wown[lane, at, :]).astype(BF16)
-        place = out.at[at, pl.ds(my_quarter, quarter)]
-        for lane in range(2):
-            done['up', lane, j] = remote(fin.at[lane, at], place, dev_y(1, lane == 1))
-            done['down', lane, j] = remote(fin.at[lane, at], place, dev_y(-1, lane == 1))
-        done['own', j] = local(fin.at[0, at], place)
-        done['pair', j] = remote(fin.at[1, at], place, partner)
+        share_rows(j, at, 0, xcols)
 
     def stage_relay(j):
-        at = sub_rows(j)
-        done['up', 0, j].wait_recv()
-        cols = pl.ds(pl.multiple_of(my_half + lax.rem(y - 1 + ny, ny) * quarter, quarter), quarter)
-        done['up2', j] = remote(out.at[at, cols], out.at[at, cols], dev_y(1))
-        done['down', 1, j].wait_recv()
-        cols = pl.ds(pl.multiple_of(other_half + lax.rem(y + 1, ny) * quarter, quarter), quarter)
-        done['down2', j] = remote(out.at[at, cols], out.at[at, cols], dev_y(-1))
-
-    for copy in res_copies:
-        copy.wait_recv() if copy.is_remote else copy.wait()
-    send_far(0)
-    send_far(1)
-    y_start(3)
-    stages = (stage_far, stage_own, stage_yfar, stage_final, stage_relay)
-    for step in range(SUBS + len(stages) - 1):
-        if step == 3:
-            w_end()
-        for lag, stage in enumerate(stages):
-            if 0 <= step - lag < SUBS:
-                stage(step - lag)
-        if step == 0:
-            y_mid(3)
-        if step == 1:
-            y_end(3)
-            rs_start('w', *w_args)
-        if step == 2:
-            rs_mid('w', *w_args)
-    for j in range(SUBS):
-        done['up', 1, j].wait_recv()
-        done['down', 0, j].wait_recv()
-        done['pair', j].wait_recv()
-        done['up2', j].wait_recv()
-        done['down2', j].wait_recv()
-        done['own', j].wait()
+        relay_rows(j, sub_rows(j), 0, xcols)
+
+    def w_share():
+        for name in ('m0', 'p1', 'p0', 'm1'):
+            wx[name].wait_recv()
+        residual_ready()
+        for lane in range(2):
+            total = wown[lane] + wplus[lane].astype(F32) + wminus[lane].astype(F32)
+            fin[lane, :, xcols:] = (xres[lane, :, xcols:].astype(F32) + total).astype(BF16)
+        share_rows('w', pl.ds(0, rows), xcols, ycols)
+
+    def w_relay():
+        relay_rows('w', pl.ds(0, rows), xcols, ycols)
+
+    actions = {'ns': near_send, 'meta': send_meta, 'A': on_piece, 'S': on_side, 'PF': prefetch, 'G': gather,
+               'U0': functools.partial(gate_up, 0), 'U1': functools.partial(gate_up, 1), 'H': share_hidden, 'T': gates, 'D': down,
+               'YS': y_start, 'YM': y_mid, 'YE': y_end, 'wf': w_far, 'WS': w_share, 'WR': w_relay,
+               'O': stage_own, 'V': stage_yfar, 'N': stage_final, 'R': stage_relay}
+    for name in ('f0', 'f1', 'm0', 'm1', 'p0', 'p1'):
+        actions[name] = functools.partial(x_send, name)
+        actions['w' + name] = functools.partial(w_send, name)
+    for name, *args in ORDER:
+        actions[name](*args)
+    for key in (*range(SUBS), 'w'):
+        done['up', 1, key].wait_recv()
+        done['down', 0, key].wait_recv()
+        done['pair', key].wait_recv()
+        done['up2', key].wait_recv()
+        done['down2', key].wait_recv()
+        done['own', key].wait()
     for copy in copies:
         if not any(copy is other for other in sent):
             copy.wait_send()
@@ -499,15 +471,15 @@
         width = w_gate.shape[2]
         capacity = (2 * rows * choice.shape[1] + experts - 1) // experts
         normed, gate_by_expert, is_chosen = norm_route(resid_in, norm_scale, w_router, choice)
-        meta = slot_meta(gate_by_expert, is_chosen, capacity)
+        meta = slot_meta(gate_by_expert, is_chosen, capacity, nx)
         half, slots = d_model // 2, 2 * capacity
         quarter = half // ny
-        ycols = 128
+        ycols = quarter // LATE_X_SHARE
         xcols = quarter - ycols
 
         hbm = pl.BlockSpec(memory_space=pl.ANY)
         out, _ = pl.pallas_call(
-            functools.partial(moe_kernel, experts, capacity, ny, nx),
+            functools.partial(moe_kernel, capacity, ny, nx),
             out_shape=(jax.ShapeDtypeStruct((rows, d_model), BF16), jax.ShapeDtypeStruct((4, 2, rows, d_model), BF16)),
             in_specs=[hbm] * 6,
             out_specs=(hbm, hbm),
@@ -539,9 +511,9 @@
                 pltpu.VMEM((2, rows, quarter), BF16),
                 pltpu.VMEM((2, rows, d_model), BF16),
                 pltpu.VMEM((2, 3, rows, 4 * capacity), BF16),
-                pltpu.VMEM((8, 2 * experts, rows), F32),
+                pltpu.VMEM((2 * nx, meta.shape[1], rows), F32),
                 pltpu.SemaphoreType.DMA((16,)),
-                pltpu.SemaphoreType.DMA((2 * (d_model // min(512, d_model)),)),
+                pltpu.SemaphoreType.DMA((2 * (d_model // min(1024, d_model)),)),
                 pltpu.SemaphoreType.DMA((256,)),
                 pltpu.SemaphoreType.DMA((256,)),
             ],

time: 176 us -> 145 us (0.82)
  Pallas kernels: 164 us -> 133 us
    pallas_call x1, Pallas kernels: 164 us -> 133 us  [device_step(): pl.pallas_call(functools.partial(moe_kernel, capacity, ny, nx), out_shape...]
where the time goes in v4:
time: 145 us
  Pallas kernels  133 us (92%)
  other arithmetic  6.03 us (4%)
  local copies, waits for them, and re-layouts  4.5 us (3%)
    pallas_call x1, Pallas kernels, device_step(): pl.pallas_call(functools.partial(moe_kernel, capacity, ny, nx), out_shape...  133 us
    unnamed x11, local copies, waits for them, and re-layouts  4.46 us

profile of v4, /device:TPU:97, one launch (start us, length us, event | category | flops | bytes accessed | tf_op | source)
XLA Modules:
  0.0 144.7 jit_solution(4802355483573708871)
XLA Ops:
  0.0 0.0 copy-start
  0.0 0.0 copy-start.3
  0.0 0.0 copy-start.2
  0.0 0.0 copy-start.4
  0.0 2.1 %convert_reduce_fusion = f32[256]{0:T(256)S(1)} fusion(bf16[256,4096]{1,0:T(8,128)(2,1)} %resid.1), kind=kLoop, calls=%fused_computation.1 | loop fusion | flops 2096896 | bytes 2098176 | tf_op jit(solution)/shard_map/reduce_sum | solution.py:35
  2.1 2.3 %fusion.2 = f32[256]{0:T(256)S(1)} fusion(bf16[256,4096]{1,0:T(8,128)(2,1)} %resid.1, f32[256]{0:T(256)S(1)} %broadcast_multiply_fusion), kind=kLoop, calls=%fused_computation.4 | loop fusion | flops 4194048 | bytes 2099200 | tf_op jit(solution)/shard_map/reduce_sum | solution.py:36
  4.4 0.0 copy-done.3
  4.4 0.0 copy-done.4
  4.5 0.0 copy-done
  4.5 0.9 fusion.4.u_in
  5.4 0.0 copy-start.1
  5.4 1.3 copy-done.1
  6.7 0.0 copy-done.2
  6.7 0.7 fusion.10
  7.5 0.2 fusion.9
  7.7 0.6 pad_maximum_fusion.meta_in
  8.4 133.2 %moe_ring.1 = (bf16[256,4096]{1,0:T(8,128)(2,1)}, bf16[4,2,256,4096]{3,2,1,0:T(8,128)(2,1)}) custom-call(bf16[256,4096]{1,0:T(8,128)(2,1)} %copy-done.1, bf16[256,4096]{1,0:T(8,128)(2,1)} %resid.1, f32[4,8,256]{2,1,0:T(8,128)} %pad_maximum_fusion.meta_in, bf16[2,4096,768]{2,1,0:T(8,128)(2,1)} %w_gate.1, bf16[2,4096,768]{2,1,0:T(8,128)(2,1)} %w_up.1, ...), custom_call_target="tpu_custom_call" | custom-call | tf_op jit(solution)/shard_map/moe_ring/pallas_call | solution.py:481
  141.6 3.1 %copy.11 = bf16[256,4096]{1,0:T(8,128)(2,1)} copy(bf16[256,4096]{1,0:T(8,128)(2,1)} %get-tuple-element.6) | data formatting | bytes 4194304
  (11 shorter events, 0.1 us)
Async XLA Ops:
  0.0 4.5 %copy-start = (bf16[256,4096]{1,0:T(8,128)(2,1)S(1)}, bf16[256,4096]{1,0:T(8,128)(2,1)}, u32[]{:S(2)}) copy-start(bf16[256,4096]{1,0:T(8,128)(2,1)} %resid.1) | copy-start | bytes 6291460
  0.0 4.4 %copy-start.3 = (s32[256,2]{0,1:T(2,128)S(1)}, s32[256,2]{0,1:T(2,128)}, u32[]{:S(2)}) copy-start(s32[256,2]{0,1:T(2,128)} %param.13) | copy-start | bytes 6148
  0.0 6.7 %copy-start.2 = (bf16[4096,16]{0,1:T(8,128)(2,1)S(1)}, bf16[4096,16]{0,1:T(8,128)(2,1)}, u32[]{:S(2)}) copy-start(bf16[4096,16]{0,1:T(8,128)(2,1)} %param.9) | copy-start | bytes 393220
  0.0 4.4 %copy-start.4 = (bf16[4096]{0:T(1024)(128)(2,1)S(1)}, bf16[4096]{0:T(1024)(128)(2,1)}, u32[]{:S(2)}) copy-start(bf16[4096]{0:T(1024)(128)(2,1)} %param.8) | copy-start | bytes 24580
  5.4 1.3 copy-start.1

commit v5 on v4

--- a/solution.py
+++ b/solution.py
@@ -15,48 +15,41 @@
 PIECES = 4
 LATE_X_SHARE = 2
 ORDER = (
-    ('ns', 2, 1), ('ns', 1, 0), ('ns', 2, 3), ('ns', 1, 2), ('G', 0), ('A', 2, 1), ('A', 1, 0), ('T', 0), ('A', 1, 2),
-    ('ns', 1, 1), ('A', 2, 3), ('ns', 1, 3), ('ns', 2, 2), ('ns', 2, 0), ('U0', 0), ('U1', 0), ('A', 3, 0), ('H', 0),
-    ('A', 3, 1), ('A', 3, 2), ('S', 1, 0), ('A', 3, 3), ('D', 0), ('S', 1, 2), ('S', 3, 0), ('S', 3, 1), ('A', 1, 1),
-    ('A', 2, 2), ('meta',), ('S', 3, 2), ('S', 3, 3), ('S', 2, 3), ('PF', 3), ('A', 2, 0), ('A', 1, 3), ('G', 3),
-    ('YS', 0), ('U0', 3), ('S', 1, 1), ('U1', 3), ('H', 3), ('T', 3), ('S', 1, 3), ('S', 2, 2), ('PF', 1), ('S', 2, 1),
-    ('D', 3), ('S', 2, 0), ('YS', 3), ('f1', 3), ('f1', 1), ('G', 1), ('PF', 2), ('U0', 1), ('T', 1), ('f0', 3),
-    ('U1', 1), ('H', 1), ('f0', 1), ('G', 2), ('f0', 2), ('f1', 0), ('D', 1), ('m0', 0), ('m0', 3), ('YS', 1),
-    ('U0', 2), ('U1', 2), ('H', 2), ('f0', 0), ('m1', 1), ('YM', 3), ('m0', 1), ('T', 2), ('f1', 2), ('D', 2),
-    ('YS', 2), ('p1', 0), ('p0', 0), ('YE', 3), ('m1', 3), ('YM', 1), ('p1', 1), ('YM', 2), ('p0', 1), ('YM', 0),
-    ('m1', 0), ('p0', 3), ('p1', 3), ('wf',), ('m0', 2), ('O', 1), ('O', 0), ('p1', 2), ('YE', 1), ('wm1',), ('m1', 2),
-    ('p0', 2), ('V', 1), ('V', 0), ('O', 3), ('N', 1), ('V', 3), ('YE', 2), ('wm0',), ('YE', 0), ('wp1',), ('N', 0),
-    ('R', 1), ('wp0',), ('N', 3), ('O', 2), ('R', 0), ('R', 3), ('V', 2), ('WS',), ('N', 2), ('WR',), ('R', 2),
+    ('ns', 1, 0), ('ns', 1, 2), ('ns', 2, 3), ('E2',), ('ns', 2, 1), ('G', 0), ('T', 0), ('A', 2, 3), ('A', 1, 0),
+    ('U0', 0), ('A', 1, 2), ('A', 2, 1), ('ns', 2, 2), ('U1', 0), ('H', 0), ('S', 1, 0), ('A', 3, 3), ('ns', 1, 1),
+    ('A', 3, 0), ('A', 3, 1), ('A', 3, 2), ('ns', 1, 3), ('D', 0), ('ns', 2, 0), ('S', 3, 3), ('A', 2, 2), ('S', 3, 0),
+    ('A', 1, 1), ('S', 3, 2), ('S', 3, 1), ('PF', 3), ('meta',), ('A', 2, 0), ('A', 1, 3), ('YS', 0), ('S', 2, 1),
+    ('G', 3), ('U0', 3), ('S', 1, 2), ('S', 1, 1), ('U1', 3), ('H', 3), ('T', 3), ('S', 1, 3), ('PF', 1), ('S', 2, 2),
+    ('S', 2, 0), ('D', 3), ('f1', 2), ('YS', 3), ('f0', 2), ('S', 2, 3), ('f0', 3), ('f1', 1), ('G', 1), ('U0', 1),
+    ('PF', 2), ('T', 1), ('U1', 1), ('H', 1), ('YM', 3), ('f0', 1), ('f1', 0), ('f1', 3), ('G', 2), ('D', 1), ('YS', 1),
+    ('m0', 0), ('f0', 0), ('U0', 2), ('U1', 2), ('H', 2), ('YM', 0), ('T', 2), ('YE', 3), ('m0', 1), ('wf',), ('D', 2),
+    ('p1', 0), ('m1', 0), ('YS', 2), ('p0', 0), ('p1', 1), ('m1', 2), ('p0', 1), ('YM', 2), ('O', 0), ('m1', 1),
+    ('p1', 2), ('p0', 2), ('YM', 1), ('m0', 2), ('m1', 3), ('V', 0), ('O', 1), ('p0', 3), ('N', 0), ('YE', 2), ('V', 1),
+    ('YE', 1), ('p1', 3), ('O', 2), ('wp0',), ('m0', 3), ('wp1',), ('N', 1), ('wm0',), ('R', 0), ('wm1',), ('V', 2),
+    ('O', 3), ('R', 1), ('N', 2), ('V', 3), ('YE', 0), ('WS',), ('R', 2), ('N', 3), ('WR',), ('R', 3),
 )
 
 
-def norm_route(resid_rows, norm_scale, w_router, choice_rows):
-    rows_f32 = resid_rows.astype(F32)
-    centered = rows_f32 - jnp.mean(rows_f32, axis=-1, keepdims=True)
-    variance = jnp.mean(centered * centered, axis=-1, keepdims=True)
-    normed = (centered * lax.rsqrt(variance + NORM_EPS) * norm_scale.astype(F32)).astype(BF16)
-    logits = jnp.dot(normed, w_router, preferred_element_type=F32)
-    router_probs = jax.nn.softmax(logits, axis=-1)
-    expert_ids = jnp.arange(w_router.shape[1], dtype=jnp.int32)
-    chosen = choice_rows[:, :, None] == expert_ids[None, None, :]
-    picked = jnp.sum(jnp.where(chosen, router_probs[:, None, :], 0.0), axis=-1)
-    gate_vals = picked / jnp.sum(picked, axis=-1, keepdims=True)
-    gate_by_expert = jnp.sum(jnp.where(chosen, gate_vals[:, :, None], 0.0), axis=1)
-    return normed, gate_by_expert, jnp.any(chosen, axis=1)
-
-
-def slot_meta(gate_by_expert, is_chosen, capacity, chips):
-    rows = is_chosen.shape[0]
-    earlier = jnp.arange(rows)[:, None] > jnp.arange(rows)[None, :]
-    position = jnp.dot(earlier.astype(BF16), is_chosen.astype(BF16), preferred_element_type=F32)
-    kept = is_chosen & (position < capacity)
-    slots = jnp.where(kept, position, -1.0).T.reshape(chips, -1, rows)
-    gates = jnp.where(kept, gate_by_expert, 0.0).T.reshape(chips, -1, rows)
-    return jnp.concatenate([slots, gates], axis=1)
-
-
-def moe_kernel(capacity, ny, nx, u_in, resid, meta_in, w_gate, w_up, w_down, out, ug,
-               w1, v1, w2, xg, hid, hpart, sums, rfar, rplus, rminus, yown, yfar, yplus, yminus, ycon, vfar, vplus, vminus, wsum, wown, wfar, wplus, wminus, fin, xres, utile, gsplit, meta,
+def route(normed, router_t, choice_t, capacity):
+    logits = lax.dot_general(router_t, normed, (((1,), (1,)), ((), ())), preferred_element_type=F32)
+    weights = jnp.exp(logits - jnp.max(logits, axis=0, keepdims=True))
+    probs = weights / jnp.sum(weights, axis=0, keepdims=True)
+    expert_ids = lax.broadcasted_iota(jnp.int32, logits.shape, 0)
+    chosen = [expert_ids == choice_t[k:k + 1] for k in range(2)]
+    picked = [jnp.sum(jnp.where(hit, probs, 0.0), axis=0, keepdims=True) for hit in chosen]
+    total = picked[0] + picked[1]
+    gate = jnp.where(chosen[0], picked[0] / total, jnp.where(chosen[1], picked[1] / total, 0.0))
+    any_chosen = jnp.where(chosen[0], 1.0, jnp.where(chosen[1], 1.0, 0.0))
+    rows = normed.shape[0]
+    earlier = lax.broadcasted_iota(jnp.int32, (rows, rows), 0) < lax.broadcasted_iota(jnp.int32, (rows, rows), 1)
+    earlier = jnp.where(earlier, 1.0, 0.0).astype(BF16)
+    position = jnp.dot(any_chosen.astype(BF16), earlier, preferred_element_type=F32)
+    kept = (any_chosen > 0.0) & (position < capacity)
+    return jnp.where(kept, position, -1.0), jnp.where(kept, gate, 0.0)
+
+
+def moe_kernel(capacity, ny, nx, resid, scale, router_t, choice_t, w_gate, w_up, w_down, out, ug,
+               w1, v1, w2, xg, hid, hpart, sums, rfar, rplus, rminus, yown, yfar, yplus, yminus, ycon, vfar, vplus, vminus, wsum, wown, wfar, wplus, wminus, fin, xres, utile, gsplit, meta, meta_src,
                load_sem, tile_sem, send_sem, recv_sem):
     rows, d_model = resid.shape
     half = d_model // 2
@@ -80,6 +73,8 @@
 
     partner = dev_x(0, True)
 
+    first_load = pltpu.make_async_copy(resid, utile.at[0], load_sem.at[15])
+    first_load.start()
     barrier = pltpu.get_barrier_semaphore()
     peers = [dev_x(dx, o) for dx in range(nx) for o in (False, True) if (dx, o) != (0, False)]
     peers += [dev_y(dy, o) for dy in (1, -1) for o in (False, True)]
@@ -121,25 +116,46 @@
         side = parity if mine else 1 - parity
         return pl.ds(pl.multiple_of(side * (rows // 2) + q * chunk, chunk), chunk)
 
+    loads = {}
+    for e in range(2):
+        loads[e] = (local(w_gate.at[e], w1.at[e]), local(w_up.at[e], v1.at[e]))
+    first_load.wait()
+
+    def normalize(i, carry):
+        at = pl.ds(pl.multiple_of(i * 16, 16), 16)
+        values = utile[0, at, :].astype(F32)
+        centered = values - jnp.mean(values, axis=-1, keepdims=True)
+        variance = jnp.mean(centered * centered, axis=-1, keepdims=True)
+        utile[0, at, :] = (centered * lax.rsqrt(variance + NORM_EPS) * scale[...].astype(F32)).astype(BF16)
+        return carry
+
+    lax.fori_loop(0, rows // 16, normalize, 0)
+
     def meta_for(dx):
-        return meta_in.at[lax.rem(x + dx + nx, nx)]
+        return meta_src.at[lax.rem(x + dx + nx, nx)]
 
     ax = {}
 
     def near_send(slot, q):
-        ax[slot, q] = remote(u_in.at[piece(q)], ug.at[slot, 0, piece(q)], dev_x(1 if slot == 1 else -1))
-
-    own_rows = (local(u_in, utile.at[0]), remote(u_in, utile.at[1], partner))
-    meta_copies = {(0, 0): local(meta_for(0), meta.at[0]), (0, 1): remote(meta_for(0), meta.at[1], partner)}
+        ax[slot, q] = remote(utile.at[0, piece(q)], ug.at[slot, 0, piece(q)], dev_x(1 if slot == 1 else -1))
+
+    meta_copies, entry = {}, {}
+
+    def own_routes():
+        entry['own'] = remote(utile.at[0], utile.at[1], partner)
+        positions, gate_rows = route(utile[0], router_t[...], choice_t[...], capacity)
+        per_chip = positions.shape[0] // nx
+        for k in range(nx):
+            meta_src[k, :per_chip] = positions[k * per_chip:(k + 1) * per_chip]
+            meta_src[k, per_chip:] = gate_rows[k * per_chip:(k + 1) * per_chip]
+        meta[0] = meta_src[x]
+        meta_copies[0, 1] = remote(meta_for(0), meta.at[1], partner)
 
     def send_meta():
         for slot, dx in ((1, 1), (2, -1), (3, 2)):
             for lane in range(2):
                 meta_copies[slot, lane] = remote(meta_for(dx), meta.at[slot * 2 + lane], dev_x(dx, lane == 1))
 
-    loads = {}
-    for e in range(2):
-        loads[e] = (local(w_gate.at[e], w1.at[e]), local(w_up.at[e], v1.at[e]))
     w2_copies = [local(w_down.at[e, :, pl.ds(my_half, half)], w2.at[e]) for e in range(2)]
     w2_copies += [remote(w_down.at[e, :, pl.ds(other_half, half)], w2.at[2 + e], partner) for e in range(2)]
     res_copies = [local(resid.at[:, pl.ds(my_quarter, quarter)], xres.at[0]),
@@ -177,6 +193,11 @@
         return pltpu.make_async_copy(ug.at[slot, lane, :, cols], utile.at[lane, :, cols], tile_sem.at[lane * tiles + t])
 
     def prefetch(slot):
+        if 'own' in entry:
+            finish_send(entry.pop('own'))
+            for q in range(PIECES):
+                finish_send(ax[1, q])
+                finish_send(ax[2, q])
         for copy in pushed[slot]:
             copy.wait_recv()
         for t in range(tiles):
@@ -202,13 +223,12 @@
     def gather(slot):
         picks = []
         for lane in range(2):
-            copy = meta_copies[slot, lane]
-            copy.wait_recv() if copy.is_remote else copy.wait()
+            if (slot, lane) != (0, 0):
+                meta_copies[slot, lane].wait_recv()
             parts = [slot_onehot(meta_rows(slot, lane, e)[0]).astype(F32).astype(BF16) for e in range(2)]
             picks.append(jnp.concatenate(parts, axis=0))
         if slot == 0:
-            own_rows[0].wait()
-            own_rows[1].wait_recv()
+            entry['own'].wait_recv()
 
         def body(t, carry):
             cols = pl.ds(pl.multiple_of(t * tile, tile), tile)
@@ -440,7 +460,7 @@
     def w_relay():
         relay_rows('w', pl.ds(0, rows), xcols, ycols)
 
-    actions = {'ns': near_send, 'meta': send_meta, 'A': on_piece, 'S': on_side, 'PF': prefetch, 'G': gather,
+    actions = {'E2': own_routes, 'ns': near_send, 'meta': send_meta, 'A': on_piece, 'S': on_side, 'PF': prefetch, 'G': gather,
                'U0': functools.partial(gate_up, 0), 'U1': functools.partial(gate_up, 1), 'H': share_hidden, 'T': gates, 'D': down,
                'YS': y_start, 'YM': y_mid, 'YE': y_end, 'wf': w_far, 'WS': w_share, 'WR': w_relay,
                'O': stage_own, 'V': stage_yfar, 'N': stage_final, 'R': stage_relay}
@@ -470,18 +490,16 @@
         experts = w_router.shape[1]
         width = w_gate.shape[2]
         capacity = (2 * rows * choice.shape[1] + experts - 1) // experts
-        normed, gate_by_expert, is_chosen = norm_route(resid_in, norm_scale, w_router, choice)
-        meta = slot_meta(gate_by_expert, is_chosen, capacity, nx)
         half, slots = d_model // 2, 2 * capacity
         quarter = half // ny
         ycols = quarter // LATE_X_SHARE
         xcols = quarter - ycols
 
-        hbm = pl.BlockSpec(memory_space=pl.ANY)
+        hbm, vmem = pl.BlockSpec(memory_space=pl.ANY), pl.BlockSpec(memory_space=pltpu.VMEM)
         out, _ = pl.pallas_call(
             functools.partial(moe_kernel, capacity, ny, nx),
             out_shape=(jax.ShapeDtypeStruct((rows, d_model), BF16), jax.ShapeDtypeStruct((4, 2, rows, d_model), BF16)),
-            in_specs=[hbm] * 6,
+            in_specs=[hbm, vmem, vmem, vmem, hbm, hbm, hbm],
             out_specs=(hbm, hbm),
             scratch_shapes=[
                 pltpu.VMEM((2, d_model, width), BF16),
@@ -511,7 +529,8 @@
                 pltpu.VMEM((2, rows, quarter), BF16),
                 pltpu.VMEM((2, rows, d_model), BF16),
                 pltpu.VMEM((2, 3, rows, 4 * capacity), BF16),
-                pltpu.VMEM((2 * nx, meta.shape[1], rows), F32),
+                pltpu.VMEM((2 * nx, 2 * experts // nx, rows), F32),
+                pltpu.VMEM((nx, 2 * experts // nx, rows), F32),
                 pltpu.SemaphoreType.DMA((16,)),
                 pltpu.SemaphoreType.DMA((2 * (d_model // min(1024, d_model)),)),
                 pltpu.SemaphoreType.DMA((256,)),
@@ -519,7 +538,7 @@
             ],
             compiler_params=pltpu.CompilerParams(collective_id=0, has_side_effects=True, vmem_limit_bytes=67043328),
             name='moe_ring',
-        )(normed, resid_in, meta, w_gate, w_up, w_down)
+        )(resid_in, norm_scale[None, :], w_router.T, choice.T, w_gate, w_up, w_down)
         return out
 
     return jax.shard_map(device_step, mesh=mesh, in_specs=(row_spec, P(None), P(None, None), P('ep', None, 'tp'), P('ep', None, 'tp'), P('ep', 'tp', None), row_spec), out_specs=row_spec, check_vma=False)

time: 145 us -> 147 us (1.014)
  Pallas kernels: 133 us -> 142 us
  other arithmetic: 6.03 us -> 0 us
    pallas_call x1, Pallas kernels: 133 us -> 142 us  [device_step(): pl.pallas_call(functools.partial(moe_kernel, capacity, ny, nx), out_shape...]
    reduce_sum x5 -> x0, other arithmetic: 4.44 us -> none  [the longest x1 2.28 us: norm_route(): variance = jnp.mean(centered * centered, axis=-1, keepdims=True)]
    unnamed x11 -> x1, local copies, waits for them, and re-layouts: 4.46 us -> 3.13 us
where the time goes in v5:
time: 147 us
  Pallas kernels  142 us (97%)
  local copies, waits for them, and re-layouts  4.44 us (3%)
    pallas_call x1, Pallas kernels, device_step(): pl.pallas_call(functools.partial(moe_kernel, capacity, ny, nx), out_shape...  142 us
    unnamed x1, local copies, waits for them, and re-layouts  3.13 us

profile of v5, /device:TPU:97, one launch (start us, length us, event | category | flops | bytes accessed | tf_op | source)
XLA Modules:
  0.0 146.9 jit_solution(14345487736318480884)
XLA Ops:
  0.0 1.3 broadcast_in_dim.3.scale
  1.3 142.4 %moe_ring.1 = (bf16[256,4096]{1,0:T(8,128)(2,1)}, bf16[4,2,256,4096]{3,2,1,0:T(8,128)(2,1)}) custom-call(bf16[256,4096]{1,0:T(8,128)(2,1)} %resid.1, bf16[1,4096]{1,0:T(2,128)(2,1)} %broadcast_in_dim.3.scale, bf16[16,4096]{1,0:T(8,128)(2,1)} %bitcast.2, s32[2,256]{1,0:T(2,128)} %bitcast.3, bf16[2,4096,768]{2,1,0:T(8,128)(2,1)} %w_gate.1, ...), custom_call_target="tpu_custom_call" | custom-call | tf_op jit(solution)/shard_map/moe_ring/pallas_call | solution.py:499
  143.7 3.1 %copy.9 = bf16[256,4096]{1,0:T(8,128)(2,1)} copy(bf16[256,4096]{1,0:T(8,128)(2,1)} %get-tuple-element.6) | data formatting | bytes 4194304

commit v6 on v5

--- a/solution.py
+++ b/solution.py
@@ -15,18 +15,19 @@
 PIECES = 4
 LATE_X_SHARE = 2
 ORDER = (
-    ('ns', 1, 0), ('ns', 1, 2), ('ns', 2, 3), ('E2',), ('ns', 2, 1), ('G', 0), ('T', 0), ('A', 2, 3), ('A', 1, 0),
-    ('U0', 0), ('A', 1, 2), ('A', 2, 1), ('ns', 2, 2), ('U1', 0), ('H', 0), ('S', 1, 0), ('A', 3, 3), ('ns', 1, 1),
-    ('A', 3, 0), ('A', 3, 1), ('A', 3, 2), ('ns', 1, 3), ('D', 0), ('ns', 2, 0), ('S', 3, 3), ('A', 2, 2), ('S', 3, 0),
-    ('A', 1, 1), ('S', 3, 2), ('S', 3, 1), ('PF', 3), ('meta',), ('A', 2, 0), ('A', 1, 3), ('YS', 0), ('S', 2, 1),
-    ('G', 3), ('U0', 3), ('S', 1, 2), ('S', 1, 1), ('U1', 3), ('H', 3), ('T', 3), ('S', 1, 3), ('PF', 1), ('S', 2, 2),
-    ('S', 2, 0), ('D', 3), ('f1', 2), ('YS', 3), ('f0', 2), ('S', 2, 3), ('f0', 3), ('f1', 1), ('G', 1), ('U0', 1),
-    ('PF', 2), ('T', 1), ('U1', 1), ('H', 1), ('YM', 3), ('f0', 1), ('f1', 0), ('f1', 3), ('G', 2), ('D', 1), ('YS', 1),
-    ('m0', 0), ('f0', 0), ('U0', 2), ('U1', 2), ('H', 2), ('YM', 0), ('T', 2), ('YE', 3), ('m0', 1), ('wf',), ('D', 2),
-    ('p1', 0), ('m1', 0), ('YS', 2), ('p0', 0), ('p1', 1), ('m1', 2), ('p0', 1), ('YM', 2), ('O', 0), ('m1', 1),
-    ('p1', 2), ('p0', 2), ('YM', 1), ('m0', 2), ('m1', 3), ('V', 0), ('O', 1), ('p0', 3), ('N', 0), ('YE', 2), ('V', 1),
-    ('YE', 1), ('p1', 3), ('O', 2), ('wp0',), ('m0', 3), ('wp1',), ('N', 1), ('wm0',), ('R', 0), ('wm1',), ('V', 2),
-    ('O', 3), ('R', 1), ('N', 2), ('V', 3), ('YE', 0), ('WS',), ('R', 2), ('N', 3), ('WR',), ('R', 3),
+    ('ns', 2, 3), ('ns', 1, 0), ('ns', 2, 1), ('E2',), ('ns', 1, 2), ('G', 0), ('A', 1, 0), ('A', 2, 3), ('T', 0),
+    ('U0', 0), ('U1', 0), ('A', 1, 2), ('A', 2, 1), ('S', 2, 3), ('A', 3, 3), ('H', 0), ('ns', 2, 0), ('A', 3, 0),
+    ('ns', 1, 1), ('ns', 2, 2), ('D', 0), ('A', 3, 2), ('ns', 1, 3), ('meta',), ('A', 3, 1), ('S', 3, 0), ('A', 2, 0),
+    ('S', 3, 3), ('A', 1, 1), ('S', 3, 2), ('S', 3, 1), ('S', 2, 1), ('PF', 3), ('A', 1, 3), ('A', 2, 2), ('G', 3),
+    ('S', 2, 0), ('S', 1, 1), ('S', 1, 2), ('YS', 0), ('U0', 3), ('S', 1, 0), ('U1', 3), ('H', 3), ('T', 3),
+    ('S', 1, 3), ('PF', 1), ('D', 3), ('f1', 2), ('f1', 0), ('YS', 3), ('f0', 3), ('S', 2, 2), ('G', 1), ('f0', 0),
+    ('U0', 1), ('f1', 3), ('PF', 2), ('f0', 1), ('T', 1), ('U1', 1), ('H', 1), ('YM', 3), ('G', 2), ('f1', 1),
+    ('f0', 2), ('D', 1), ('m0', 0), ('YS', 1), ('U0', 2), ('U1', 2), ('H', 2), ('YE', 3), ('wf',), ('YM', 0), ('m1', 2),
+    ('T', 2), ('D', 2), ('p1', 0), ('YS', 2), ('m1', 0), ('p0', 1), ('p1', 1), ('m1', 1), ('m0', 1), ('m0', 2),
+    ('p0', 0), ('YM', 2), ('YM', 1), ('p1', 3), ('O', 1), ('YE', 2), ('wp1',), ('O', 0), ('wp0',), ('YE', 1), ('wm1',),
+    ('wm0',), ('V', 1), ('m1', 3), ('m0', 3), ('V', 0), ('p0', 3), ('N', 1), ('p0', 2), ('N', 0), ('YE', 0), ('WS',),
+    ('p1', 2), ('O', 3), ('O', 2), ('V', 3), ('R', 0), ('V', 2), ('R', 1), ('N', 3), ('N', 2), ('WR',), ('R', 3),
+    ('R', 2),
 )
 
 
@@ -116,10 +117,10 @@
         side = parity if mine else 1 - parity
         return pl.ds(pl.multiple_of(side * (rows // 2) + q * chunk, chunk), chunk)
 
+    first_load.wait()
     loads = {}
     for e in range(2):
         loads[e] = (local(w_gate.at[e], w1.at[e]), local(w_up.at[e], v1.at[e]))
-    first_load.wait()
 
     def normalize(i, carry):
         at = pl.ds(pl.multiple_of(i * 16, 16), 16)
@@ -139,10 +140,11 @@
     def near_send(slot, q):
         ax[slot, q] = remote(utile.at[0, piece(q)], ug.at[slot, 0, piece(q)], dev_x(1 if slot == 1 else -1))
 
-    meta_copies, entry = {}, {}
+    meta_copies, entry, w2_copies, res_copies = {}, {}, [], []
 
     def own_routes():
         entry['own'] = remote(utile.at[0], utile.at[1], partner)
+        w2_copies.extend(local(w_down.at[e, :, pl.ds(my_half, half)], w2.at[e]) for e in range(2))
         positions, gate_rows = route(utile[0], router_t[...], choice_t[...], capacity)
         per_chip = positions.shape[0] // nx
         for k in range(nx):
@@ -150,16 +152,14 @@
             meta_src[k, per_chip:] = gate_rows[k * per_chip:(k + 1) * per_chip]
         meta[0] = meta_src[x]
         meta_copies[0, 1] = remote(meta_for(0), meta.at[1], partner)
+        w2_copies.extend(remote(w_down.at[e, :, pl.ds(other_half, half)], w2.at[2 + e], partner) for e in range(2))
+        res_copies.append(local(resid.at[:, pl.ds(my_quarter, quarter)], xres.at[0]))
+        res_copies.append(remote(resid.at[:, pl.ds(other_quarter, quarter)], xres.at[1], partner))
 
     def send_meta():
         for slot, dx in ((1, 1), (2, -1), (3, 2)):
             for lane in range(2):
                 meta_copies[slot, lane] = remote(meta_for(dx), meta.at[slot * 2 + lane], dev_x(dx, lane == 1))
-
-    w2_copies = [local(w_down.at[e, :, pl.ds(my_half, half)], w2.at[e]) for e in range(2)]
-    w2_copies += [remote(w_down.at[e, :, pl.ds(other_half, half)], w2.at[2 + e], partner) for e in range(2)]
-    res_copies = [local(resid.at[:, pl.ds(my_quarter, quarter)], xres.at[0]),
-                  remote(resid.at[:, pl.ds(other_quarter, quarter)], xres.at[1], partner)]
 
     ay, pushed = {}, {1: [], 2: [], 3: []}
 

time: 147 us -> 141 us (0.959)
  Pallas kernels: 142 us -> 136 us
    pallas_call x1, Pallas kernels: 142 us -> 136 us  [device_step(): pl.pallas_call(functools.partial(moe_kernel, capacity, ny, nx), out_shape...]
where the time goes in v6:
time: 141 us; the launch traced here: 140 us
  Pallas kernels  136 us (96%)
  local copies, waits for them, and re-layouts  4.44 us (3%)
    pallas_call x1, Pallas kernels, device_step(): pl.pallas_call(functools.partial(moe_kernel, capacity, ny, nx), out_shape...  136 us
    unnamed x1, local copies, waits for them, and re-layouts  3.13 us

profile of v6, /device:TPU:97, one launch (start us, length us, event | category | flops | bytes accessed | tf_op | source)
XLA Modules:
  0.0 140.4 jit_solution(3838898803530806259)
XLA Ops:
  0.0 1.3 broadcast_in_dim.3.scale
  1.3 136.0 %moe_ring.1 = (bf16[256,4096]{1,0:T(8,128)(2,1)}, bf16[4,2,256,4096]{3,2,1,0:T(8,128)(2,1)}) custom-call(bf16[256,4096]{1,0:T(8,128)(2,1)} %resid.1, bf16[1,4096]{1,0:T(2,128)(2,1)} %broadcast_in_dim.3.scale, bf16[16,4096]{1,0:T(8,128)(2,1)} %bitcast.2, s32[2,256]{1,0:T(2,128)} %bitcast.3, bf16[2,4096,768]{2,1,0:T(8,128)(2,1)} %w_gate.1, ...), custom_call_target="tpu_custom_call" | custom-call | tf_op jit(solution)/shard_map/moe_ring/pallas_call | solution.py:499
  137.3 3.1 %copy.9 = bf16[256,4096]{1,0:T(8,128)(2,1)} copy(bf16[256,4096]{1,0:T(8,128)(2,1)} %get-tuple-element.6) | data formatting | bytes 4194304

commit v7 on v6

--- a/solution.py
+++ b/solution.py
@@ -50,7 +50,7 @@
 
 
 def moe_kernel(capacity, ny, nx, resid, scale, router_t, choice_t, w_gate, w_up, w_down, out, ug,
-               w1, v1, w2, xg, hid, hpart, sums, rfar, rplus, rminus, yown, yfar, yplus, yminus, ycon, vfar, vplus, vminus, wsum, wown, wfar, wplus, wminus, fin, xres, utile, gsplit, meta, meta_src,
+               w1, v1, w2, xg, hid, hpart, sums, rfar, rplus, rminus, yown, yfar, yplus, yminus, ycon, vfar, vplus, vminus, wsum, wown, wfar, wplus, wminus, fin, xres, utile, select, gate_col, meta, meta_src,
                load_sem, tile_sem, send_sem, recv_sem):
     rows, d_model = resid.shape
     half = d_model // 2
@@ -122,12 +122,14 @@
     for e in range(2):
         loads[e] = (local(w_gate.at[e], w1.at[e]), local(w_up.at[e], v1.at[e]))
 
+    gain = scale[...].astype(F32)[None, :]
+
     def normalize(i, carry):
         at = pl.ds(pl.multiple_of(i * 16, 16), 16)
         values = utile[0, at, :].astype(F32)
         centered = values - jnp.mean(values, axis=-1, keepdims=True)
         variance = jnp.mean(centered * centered, axis=-1, keepdims=True)
-        utile[0, at, :] = (centered * lax.rsqrt(variance + NORM_EPS) * scale[...].astype(F32)).astype(BF16)
+        utile[0, at, :] = (centered * lax.rsqrt(variance + NORM_EPS) * gain).astype(BF16)
         return carry
 
     lax.fori_loop(0, rows // 16, normalize, 0)
@@ -210,15 +212,21 @@
 
     def gates(slot):
         for lane in range(2):
-            parts = []
+            taken = jnp.zeros((1, rows), F32)
+            picks, weights = ([], []), [jnp.zeros((1, rows), F32), jnp.zeros((1, rows), F32)]
             for e in range(4):
                 pos_row, gate_row = meta_rows(slot, lane, e)
-                parts.append(jnp.where(slot_onehot(pos_row), gate_row, 0.0))
-            gate_mat = jnp.concatenate(parts, axis=0).T
-            for term in range(3):
-                part = gate_mat.astype(BF16)
-                gsplit[lane, term] = part
-                gate_mat = gate_mat - part.astype(F32)
+                hit = slot_onehot(pos_row)
+                for k in range(2):
+                    here = taken == float(k)
+                    picks[k].append(jnp.where(hit, jnp.where(here, 1.0, 0.0), 0.0))
+                    weights[k] = weights[k] + jnp.where(here, jnp.where(pos_row >= 0.0, gate_row, 0.0), 0.0)
+                taken = taken + jnp.where(pos_row >= 0.0, 1.0, 0.0)
+            for k in range(2):
+                select[lane, k] = jnp.concatenate(picks[k], axis=0).T.astype(BF16)
+            columns = jnp.concatenate([*weights, jnp.zeros((6, rows), F32)], axis=0).T
+            for k in range(2):
+                gate_col[lane, k] = jnp.broadcast_to(columns[:, k:k + 1], gate_col.shape[2:])
 
     def gather(slot):
         picks = []
@@ -284,9 +292,8 @@
                     at = lane if e < 2 else 1 - lane
                     stack.append(outs[e][at * capacity:(at + 1) * capacity])
                 stacked = jnp.concatenate(stack, axis=0)
-                total = jnp.dot(gsplit[lane, 0], stacked, preferred_element_type=F32)
-                for term in (1, 2):
-                    total += jnp.dot(gsplit[lane, term], stacked, preferred_element_type=F32)
+                total = jnp.dot(select[lane, 0], stacked, preferred_element_type=F32) * gate_col[lane, 0][:, :1]
+                total += jnp.dot(select[lane, 1], stacked, preferred_element_type=F32) * gate_col[lane, 1][:, :1]
                 total = total.astype(BF16)
                 sums[slot, lane, :, pl.ds(pl.multiple_of(t * xcols, 128), xcols)] = total[:, :xcols]
                 ycon[slot, lane, :, pl.ds(pl.multiple_of(t * ycols, 128), ycols)] = total[:, xcols:]
@@ -528,7 +535,8 @@
                 pltpu.VMEM((2, rows, quarter), BF16),
                 pltpu.VMEM((2, rows, quarter), BF16),
                 pltpu.VMEM((2, rows, d_model), BF16),
-                pltpu.VMEM((2, 3, rows, 4 * capacity), BF16),
+                pltpu.VMEM((2, 2, rows, 4 * capacity), BF16),
+                pltpu.VMEM((2, 2, rows, 128), F32),
                 pltpu.VMEM((2 * nx, 2 * experts // nx, rows), F32),
                 pltpu.VMEM((nx, 2 * experts // nx, rows), F32),
                 pltpu.SemaphoreType.DMA((16,)),
@@ -538,7 +546,7 @@
             ],
             compiler_params=pltpu.CompilerParams(collective_id=0, has_side_effects=True, vmem_limit_bytes=67043328),
             name='moe_ring',
-        )(resid_in, norm_scale[None, :], w_router.T, choice.T, w_gate, w_up, w_down)
-        return out
+        )(resid_in, norm_scale, w_router.T, choice.T, w_gate, w_up, w_down)
+        return jnp.where(choice[:, :1] >= 0, out, jnp.zeros((), BF16))
 
     return jax.shard_map(device_step, mesh=mesh, in_specs=(row_spec, P(None), P(None, None), P('ep', None, 'tp'), P('ep', None, 'tp'), P('ep', 'tp', None), row_spec), out_specs=row_spec, check_vma=False)

time: 141 us -> 139 us (0.986)
  local copies, waits for them, and re-layouts: 4.44 us -> 0 us
  other arithmetic: 0 us -> 3.82 us
    unnamed x1 -> x0, local copies, waits for them, and re-layouts: 3.13 us -> none
    select_n x0 -> x1, other arithmetic: none -> 3.12 us  [device_step(): return jnp.where(choice[:, :1] >= 0, out, jnp.zeros((), BF16))]
where the time goes in v7:
time: 139 us
  Pallas kernels  135 us (97%)
  other arithmetic  3.82 us (3%)
    pallas_call x1, Pallas kernels, device_step(): pl.pallas_call(functools.partial(moe_kernel, capacity, ny, nx), out_shape...  135 us
    select_n x1, other arithmetic, device_step(): return jnp.where(choice[:, :1] >= 0, out, jnp.zeros((), BF16))  3.12 us

profile of v7, /device:TPU:97, one launch (start us, length us, event | category | flops | bytes accessed | tf_op | source)
XLA Modules:
  0.0 138.7 jit_solution(9849668040067517234)
XLA Ops:
  0.0 134.8 %moe_ring.1 = (bf16[256,4096]{1,0:T(8,128)(2,1)}, bf16[4,2,256,4096]{3,2,1,0:T(8,128)(2,1)}) custom-call(bf16[256,4096]{1,0:T(8,128)(2,1)} %resid.1, bf16[4096]{0:T(1024)(128)(2,1)} %scale.1, bf16[16,4096]{1,0:T(8,128)(2,1)} %bitcast.2, s32[2,256]{1,0:T(2,128)} %bitcast.3, bf16[2,4096,768]{2,1,0:T(8,128)(2,1)} %w_gate.1, bf16[2,4096,768]{2,1,0:T(8,128)(2,1)} %w_up.1, ...), custom_call_target="tpu_custom_call" | custom-call | tf_op jit(solution)/shard_map/moe_ring/pallas_call | solution.py:506
  134.8 0.7 compare_reduce_fusion
  135.6 3.1 %broadcast_select_fusion = bf16[256,4096]{1,0:T(8,128)(2,1)} fusion(bf16[256,4096]{1,0:T(8,128)(2,1)} %get-tuple-element.6, pred[256]{0:T(512)(128)(4,1)S(1)} %compare_reduce_fusion), kind=kLoop, calls=%fused_computation | loop fusion | flops 1048576 | bytes 4194560 | tf_op jit(solution)/shard_map/jit(_where)/select_n | solution.py:550

commit v8 on v7

--- a/solution.py
+++ b/solution.py
@@ -15,18 +15,18 @@
 PIECES = 4
 LATE_X_SHARE = 2
 ORDER = (
-    ('ns', 2, 3), ('ns', 1, 0), ('ns', 2, 1), ('E2',), ('ns', 1, 2), ('G', 0), ('A', 1, 0), ('A', 2, 3), ('T', 0),
-    ('U0', 0), ('U1', 0), ('A', 1, 2), ('A', 2, 1), ('S', 2, 3), ('A', 3, 3), ('H', 0), ('ns', 2, 0), ('A', 3, 0),
-    ('ns', 1, 1), ('ns', 2, 2), ('D', 0), ('A', 3, 2), ('ns', 1, 3), ('meta',), ('A', 3, 1), ('S', 3, 0), ('A', 2, 0),
-    ('S', 3, 3), ('A', 1, 1), ('S', 3, 2), ('S', 3, 1), ('S', 2, 1), ('PF', 3), ('A', 1, 3), ('A', 2, 2), ('G', 3),
-    ('S', 2, 0), ('S', 1, 1), ('S', 1, 2), ('YS', 0), ('U0', 3), ('S', 1, 0), ('U1', 3), ('H', 3), ('T', 3),
-    ('S', 1, 3), ('PF', 1), ('D', 3), ('f1', 2), ('f1', 0), ('YS', 3), ('f0', 3), ('S', 2, 2), ('G', 1), ('f0', 0),
-    ('U0', 1), ('f1', 3), ('PF', 2), ('f0', 1), ('T', 1), ('U1', 1), ('H', 1), ('YM', 3), ('G', 2), ('f1', 1),
-    ('f0', 2), ('D', 1), ('m0', 0), ('YS', 1), ('U0', 2), ('U1', 2), ('H', 2), ('YE', 3), ('wf',), ('YM', 0), ('m1', 2),
-    ('T', 2), ('D', 2), ('p1', 0), ('YS', 2), ('m1', 0), ('p0', 1), ('p1', 1), ('m1', 1), ('m0', 1), ('m0', 2),
-    ('p0', 0), ('YM', 2), ('YM', 1), ('p1', 3), ('O', 1), ('YE', 2), ('wp1',), ('O', 0), ('wp0',), ('YE', 1), ('wm1',),
-    ('wm0',), ('V', 1), ('m1', 3), ('m0', 3), ('V', 0), ('p0', 3), ('N', 1), ('p0', 2), ('N', 0), ('YE', 0), ('WS',),
-    ('p1', 2), ('O', 3), ('O', 2), ('V', 3), ('R', 0), ('V', 2), ('R', 1), ('N', 3), ('N', 2), ('WR',), ('R', 3),
+    ('ns', 1, 0), ('ns', 2, 3), ('ns', 2, 1), ('ns', 1, 2), ('E2',), ('A', 1, 0), ('A', 2, 3), ('A', 1, 2), ('A', 2, 1),
+    ('G', 0), ('ns', 2, 0), ('ns', 2, 2), ('U0', 0), ('S', 2, 3), ('A', 3, 0), ('ns', 1, 3), ('A', 3, 3), ('U1', 0),
+    ('H', 0), ('A', 3, 2), ('A', 3, 1), ('ns', 1, 1), ('S', 3, 3), ('S', 3, 0), ('T', 0), ('D', 0), ('A', 1, 3),
+    ('meta',), ('A', 2, 0), ('S', 3, 2), ('S', 3, 1), ('PF', 3), ('S', 2, 1), ('S', 1, 2), ('S', 1, 0), ('A', 1, 1),
+    ('A', 2, 2), ('G', 3), ('U0', 3), ('YS', 0), ('S', 1, 3), ('U1', 3), ('H', 3), ('S', 1, 1), ('T', 3), ('PF', 1),
+    ('S', 2, 2), ('D', 3), ('f0', 2), ('f1', 0), ('f1', 2), ('f1', 3), ('YS', 3), ('S', 2, 0), ('G', 1), ('PF', 2),
+    ('T', 1), ('f1', 1), ('U0', 1), ('YM', 0), ('U1', 1), ('f0', 0), ('f0', 1), ('YM', 3), ('H', 1), ('G', 2),
+    ('f0', 3), ('D', 1), ('YS', 1), ('m0', 3), ('U0', 2), ('U1', 2), ('H', 2), ('YE', 3), ('wf',), ('m0', 0), ('T', 2),
+    ('D', 2), ('p1', 3), ('m1', 3), ('m0', 1), ('YM', 1), ('p0', 3), ('p1', 0), ('m1', 0), ('p0', 0), ('YE', 0),
+    ('p1', 1), ('YS', 2), ('YE', 1), ('O', 3), ('YM', 2), ('m0', 2), ('p0', 1), ('m1', 1), ('p0', 2), ('V', 3),
+    ('m1', 2), ('O', 0), ('N', 3), ('V', 0), ('p1', 2), ('O', 1), ('N', 0), ('YE', 2), ('wp0',), ('wp1',), ('R', 3),
+    ('wm0',), ('wm1',), ('V', 1), ('R', 0), ('O', 2), ('N', 1), ('V', 2), ('WS',), ('N', 2), ('R', 1), ('WR',),
     ('R', 2),
 )
 
@@ -50,7 +50,7 @@
 
 
 def moe_kernel(capacity, ny, nx, resid, scale, router_t, choice_t, w_gate, w_up, w_down, out, ug,
-               w1, v1, w2, xg, hid, hpart, sums, rfar, rplus, rminus, yown, yfar, yplus, yminus, ycon, vfar, vplus, vminus, wsum, wown, wfar, wplus, wminus, fin, xres, utile, select, gate_col, meta, meta_src,
+               w1, v1, w2, xg, hid, hpart, sums, rfar, rplus, rminus, yown, yfar, yplus, yminus, ycon, vfar, vplus, vminus, wsum, wown, wfar, wplus, wminus, xres, utile, select, gate_col, meta, meta_src,
                load_sem, tile_sem, send_sem, recv_sem):
     rows, d_model = resid.shape
     half = d_model // 2
@@ -124,15 +124,21 @@
 
     gain = scale[...].astype(F32)[None, :]
 
-    def normalize(i, carry):
-        at = pl.ds(pl.multiple_of(i * 16, 16), 16)
+    def normalize(i, start):
+        at = pl.ds(pl.multiple_of(start + i * 16, 16), 16)
         values = utile[0, at, :].astype(F32)
         centered = values - jnp.mean(values, axis=-1, keepdims=True)
         variance = jnp.mean(centered * centered, axis=-1, keepdims=True)
         utile[0, at, :] = (centered * lax.rsqrt(variance + NORM_EPS) * gain).astype(BF16)
-        return carry
-
-    lax.fori_loop(0, rows // 16, normalize, 0)
+        return start
+
+    normalized = set()
+
+    def norm_piece(q):
+        if q not in normalized:
+            normalized.add(q)
+            lax.fori_loop(0, chunk // 16, normalize, parity * (rows // 2) + q * chunk)
+
 
     def meta_for(dx):
         return meta_src.at[lax.rem(x + dx + nx, nx)]
@@ -140,11 +146,15 @@
     ax = {}
 
     def near_send(slot, q):
+        norm_piece(q)
         ax[slot, q] = remote(utile.at[0, piece(q)], ug.at[slot, 0, piece(q)], dev_x(1 if slot == 1 else -1))
 
     meta_copies, entry, w2_copies, res_copies = {}, {}, [], []
 
     def own_routes():
+        for q in range(PIECES):
+            norm_piece(q)
+        lax.fori_loop(0, rows // 32, normalize, (1 - parity) * (rows // 2))
         entry['own'] = remote(utile.at[0], utile.at[1], partner)
         w2_copies.extend(local(w_down.at[e, :, pl.ds(my_half, half)], w2.at[e]) for e in range(2))
         positions, gate_rows = route(utile[0], router_t[...], choice_t[...], capacity)
@@ -224,9 +234,7 @@
                 taken = taken + jnp.where(pos_row >= 0.0, 1.0, 0.0)
             for k in range(2):
                 select[lane, k] = jnp.concatenate(picks[k], axis=0).T.astype(BF16)
-            columns = jnp.concatenate([*weights, jnp.zeros((6, rows), F32)], axis=0).T
-            for k in range(2):
-                gate_col[lane, k] = jnp.broadcast_to(columns[:, k:k + 1], gate_col.shape[2:])
+            gate_col[lane] = jnp.concatenate([*weights, jnp.zeros((6, rows), F32)], axis=0).T
 
     def gather(slot):
         picks = []
@@ -292,8 +300,8 @@
                     at = lane if e < 2 else 1 - lane
                     stack.append(outs[e][at * capacity:(at + 1) * capacity])
                 stacked = jnp.concatenate(stack, axis=0)
-                total = jnp.dot(select[lane, 0], stacked, preferred_element_type=F32) * gate_col[lane, 0][:, :1]
-                total += jnp.dot(select[lane, 1], stacked, preferred_element_type=F32) * gate_col[lane, 1][:, :1]
+                total = jnp.dot(select[lane, 0], stacked, preferred_element_type=F32) * gate_col[lane, :, 0:1]
+                total += jnp.dot(select[lane, 1], stacked, preferred_element_type=F32) * gate_col[lane, :, 1:2]
                 total = total.astype(BF16)
                 sums[slot, lane, :, pl.ds(pl.multiple_of(t * xcols, 128), xcols)] = total[:, :xcols]
                 ycon[slot, lane, :, pl.ds(pl.multiple_of(t * ycols, 128), ycols)] = total[:, xcols:]
@@ -424,7 +432,7 @@
         def place(start):
             return out.at[at, pl.ds(pl.multiple_of(start + first, 128), cols)]
 
-        src = fin.at[:, at, pl.ds(first, cols)]
+        src = xres.at[:, at, pl.ds(first, cols)]
         for lane in range(2):
             done['up', lane, key] = remote(src.at[lane], place(my_quarter), dev_y(1, lane == 1))
             done['down', lane, key] = remote(src.at[lane], place(my_quarter), dev_y(-1, lane == 1))
@@ -449,7 +457,7 @@
         at = sub_rows(j)
         for lane in range(2):
             total = yown[lane, at, :] + yplus[lane, at, :].astype(F32) + yminus[lane, at, :].astype(F32)
-            fin[lane, at, :xcols] = (xres[lane, at, :xcols].astype(F32) + total).astype(BF16)
+            xres[lane, at, :xcols] = (xres[lane, at, :xcols].astype(F32) + total).astype(BF16)
         share_rows(j, at, 0, xcols)
 
     def stage_relay(j):
@@ -461,7 +469,7 @@
         residual_ready()
         for lane in range(2):
             total = wown[lane] + wplus[lane].astype(F32) + wminus[lane].astype(F32)
-            fin[lane, :, xcols:] = (xres[lane, :, xcols:].astype(F32) + total).astype(BF16)
+            xres[lane, :, xcols:] = (xres[lane, :, xcols:].astype(F32) + total).astype(BF16)
         share_rows('w', pl.ds(0, rows), xcols, ycols)
 
     def w_relay():
@@ -533,10 +541,9 @@
                 pltpu.VMEM((2, rows, ycols), BF16),
                 pltpu.VMEM((2, rows, ycols), BF16),
                 pltpu.VMEM((2, rows, quarter), BF16),
-                pltpu.VMEM((2, rows, quarter), BF16),
                 pltpu.VMEM((2, rows, d_model), BF16),
                 pltpu.VMEM((2, 2, rows, 4 * capacity), BF16),
-                pltpu.VMEM((2, 2, rows, 128), F32),
+                pltpu.VMEM((2, rows, 8), F32),
                 pltpu.VMEM((2 * nx, 2 * experts // nx, rows), F32),
                 pltpu.VMEM((nx, 2 * experts // nx, rows), F32),
                 pltpu.SemaphoreType.DMA((16,)),
@@ -547,6 +554,6 @@
             compiler_params=pltpu.CompilerParams(collective_id=0, has_side_effects=True, vmem_limit_bytes=67043328),
             name='moe_ring',
         )(resid_in, norm_scale, w_router.T, choice.T, w_gate, w_up, w_down)
-        return jnp.where(choice[:, :1] >= 0, out, jnp.zeros((), BF16))
+        return out
 
     return jax.shard_map(device_step, mesh=mesh, in_specs=(row_spec, P(None), P(None, None), P('ep', None, 'tp'), P('ep', None, 'tp'), P('ep', 'tp', None), row_spec), out_specs=row_spec, check_vma=False)

time: 139 us -> 134 us (0.964)
  Pallas kernels: 135 us -> 131 us
  other arithmetic: 3.82 us -> 0 us
  local copies, waits for them, and re-layouts: 0 us -> 3.13 us
    pallas_call x1, Pallas kernels: 135 us -> 131 us  [device_step(): pl.pallas_call(functools.partial(moe_kernel, capacity, ny, nx), out_shape...]
    unnamed x0 -> x1, local copies, waits for them, and re-layouts: none -> 3.13 us
    select_n x1 -> x0, other arithmetic: 3.12 us -> none  [device_step(): return jnp.where(choice[:, :1] >= 0, out, jnp.zeros((), BF16))]
where the time goes in v8:
time: 134 us
  Pallas kernels  131 us (98%)
  local copies, waits for them, and re-layouts  3.13 us (2%)
    pallas_call x1, Pallas kernels, device_step(): pl.pallas_call(functools.partial(moe_kernel, capacity, ny, nx), out_shape...  131 us
    unnamed x1, local copies, waits for them, and re-layouts  3.13 us

profile of v8, /device:TPU:97, one launch (start us, length us, event | category | flops | bytes accessed | tf_op | source)
XLA Modules:
  0.0 134.3 jit_solution(17397536066765212404)
XLA Ops:
  0.0 131.2 %moe_ring.1 = (bf16[256,4096]{1,0:T(8,128)(2,1)}, bf16[4,2,256,4096]{3,2,1,0:T(8,128)(2,1)}) custom-call(bf16[256,4096]{1,0:T(8,128)(2,1)} %resid.1, bf16[4096]{0:T(1024)(128)(2,1)} %scale.1, bf16[16,4096]{1,0:T(8,128)(2,1)} %bitcast.2, s32[2,256]{1,0:T(2,128)} %bitcast.3, bf16[2,4096,768]{2,1,0:T(8,128)(2,1)} %w_gate.1, bf16[2,4096,768]{2,1,0:T(8,128)(2,1)} %w_up.1, ...), custom_call_target="tpu_custom_call" | custom-call | tf_op jit(solution)/shard_map/moe_ring/pallas_call | solution.py:514
  131.2 3.1 %copy.9 = bf16[256,4096]{1,0:T(8,128)(2,1)} copy(bf16[256,4096]{1,0:T(8,128)(2,1)} %get-tuple-element.6) | data formatting | bytes 4194304

commit v9 on v8

--- a/solution.py
+++ b/solution.py
@@ -15,19 +15,18 @@
 PIECES = 4
 LATE_X_SHARE = 2
 ORDER = (
-    ('ns', 1, 0), ('ns', 2, 3), ('ns', 2, 1), ('ns', 1, 2), ('E2',), ('A', 1, 0), ('A', 2, 3), ('A', 1, 2), ('A', 2, 1),
-    ('G', 0), ('ns', 2, 0), ('ns', 2, 2), ('U0', 0), ('S', 2, 3), ('A', 3, 0), ('ns', 1, 3), ('A', 3, 3), ('U1', 0),
-    ('H', 0), ('A', 3, 2), ('A', 3, 1), ('ns', 1, 1), ('S', 3, 3), ('S', 3, 0), ('T', 0), ('D', 0), ('A', 1, 3),
-    ('meta',), ('A', 2, 0), ('S', 3, 2), ('S', 3, 1), ('PF', 3), ('S', 2, 1), ('S', 1, 2), ('S', 1, 0), ('A', 1, 1),
-    ('A', 2, 2), ('G', 3), ('U0', 3), ('YS', 0), ('S', 1, 3), ('U1', 3), ('H', 3), ('S', 1, 1), ('T', 3), ('PF', 1),
-    ('S', 2, 2), ('D', 3), ('f0', 2), ('f1', 0), ('f1', 2), ('f1', 3), ('YS', 3), ('S', 2, 0), ('G', 1), ('PF', 2),
-    ('T', 1), ('f1', 1), ('U0', 1), ('YM', 0), ('U1', 1), ('f0', 0), ('f0', 1), ('YM', 3), ('H', 1), ('G', 2),
-    ('f0', 3), ('D', 1), ('YS', 1), ('m0', 3), ('U0', 2), ('U1', 2), ('H', 2), ('YE', 3), ('wf',), ('m0', 0), ('T', 2),
-    ('D', 2), ('p1', 3), ('m1', 3), ('m0', 1), ('YM', 1), ('p0', 3), ('p1', 0), ('m1', 0), ('p0', 0), ('YE', 0),
-    ('p1', 1), ('YS', 2), ('YE', 1), ('O', 3), ('YM', 2), ('m0', 2), ('p0', 1), ('m1', 1), ('p0', 2), ('V', 3),
-    ('m1', 2), ('O', 0), ('N', 3), ('V', 0), ('p1', 2), ('O', 1), ('N', 0), ('YE', 2), ('wp0',), ('wp1',), ('R', 3),
-    ('wm0',), ('wm1',), ('V', 1), ('R', 0), ('O', 2), ('N', 1), ('V', 2), ('WS',), ('N', 2), ('R', 1), ('WR',),
-    ('R', 2),
+    ('ns', 1, 0), ('ns', 2, 3), ('ns', 1, 2), ('ns', 2, 1), ('A', 1, 0), ('A', 2, 3), ('E2',), ('A', 1, 2), ('A', 2, 1),
+    ('ns', 1, 3), ('S', 2, 3), ('ns', 2, 2), ('G', 0), ('A', 3, 0), ('A', 3, 3), ('U0', 0), ('U1', 0), ('H', 0),
+    ('T', 0), ('A', 3, 2), ('A', 3, 1), ('S', 3, 3), ('ns', 1, 1), ('S', 3, 0), ('ns', 2, 0), ('D', 0), ('A', 1, 3),
+    ('S', 3, 2), ('S', 3, 1), ('PF', 3), ('A', 2, 2), ('meta',), ('S', 2, 1), ('A', 1, 1), ('G', 3), ('A', 2, 0),
+    ('S', 1, 0), ('YS', 0), ('U0', 3), ('S', 1, 3), ('S', 1, 2), ('U1', 3), ('H', 3), ('S', 1, 1), ('T', 3), ('PF', 1),
+    ('D', 3), ('f1', 0), ('f1', 3), ('YS', 3), ('S', 2, 2), ('f0', 2), ('f0', 3), ('S', 2, 0), ('f1', 1), ('G', 1),
+    ('PF', 2), ('U0', 1), ('U1', 1), ('H', 1), ('G', 2), ('YM', 3), ('f0', 0), ('T', 1), ('D', 1), ('YS', 1), ('m0', 1),
+    ('f0', 1), ('m0', 0), ('U0', 2), ('m0', 3), ('U1', 2), ('H', 2), ('YE', 3), ('wf',), ('T', 2), ('YM', 0), ('D', 2),
+    ('p1', 3), ('YS', 2), ('p0', 3), ('m1', 3), ('YE', 0), ('YM', 1), ('p0', 1), ('p1', 1), ('m1', 1), ('p1', 0),
+    ('O', 3), ('p0', 0), ('m1', 0), ('f1', 2), ('YM', 2), ('V', 3), ('O', 1), ('N', 3), ('p1', 2), ('YE', 1), ('m1', 2),
+    ('p0', 2), ('V', 1), ('O', 0), ('m0', 2), ('YE', 2), ('wp1',), ('wm1',), ('wp0',), ('N', 1), ('V', 0), ('R', 3),
+    ('R', 1), ('wm0',), ('N', 0), ('O', 2), ('R', 0), ('V', 2), ('WS',), ('N', 2), ('WR',), ('R', 2),
 )
 
 

time: 134 us -> 136 us (1.015)
  Pallas kernels: 131 us -> 133 us
    pallas_call x1, Pallas kernels: 131 us -> 133 us  [device_step(): pl.pallas_call(functools.partial(moe_kernel, capacity, ny, nx), out_shape...]
where the time goes in v9:
time: 136 us
  Pallas kernels  133 us (98%)
  local copies, waits for them, and re-layouts  3.13 us (2%)
    pallas_call x1, Pallas kernels, device_step(): pl.pallas_call(functools.partial(moe_kernel, capacity, ny, nx), out_shape...  133 us
    unnamed x1, local copies, waits for them, and re-layouts  3.13 us

profile of v9, /device:TPU:97, one launch (start us, length us, event | category | flops | bytes accessed | tf_op | source)
XLA Modules:
  0.0 136.2 jit_solution(18446488861454961627)
XLA Ops:
  0.0 133.0 %moe_ring.1 = (bf16[256,4096]{1,0:T(8,128)(2,1)}, bf16[4,2,256,4096]{3,2,1,0:T(8,128)(2,1)}) custom-call(bf16[256,4096]{1,0:T(8,128)(2,1)} %resid.1, bf16[4096]{0:T(1024)(128)(2,1)} %scale.1, bf16[16,4096]{1,0:T(8,128)(2,1)} %bitcast.2, s32[2,256]{1,0:T(2,128)} %bitcast.3, bf16[2,4096,768]{2,1,0:T(8,128)(2,1)} %w_gate.1, bf16[2,4096,768]{2,1,0:T(8,128)(2,1)} %w_up.1, ...), custom_call_target="tpu_custom_call" | custom-call | tf_op jit(solution)/shard_map/moe_ring/pallas_call | solution.py:513
  133.0 3.1 %copy.9 = bf16[256,4096]{1,0:T(8,128)(2,1)} copy(bf16[256,4096]{1,0:T(8,128)(2,1)} %get-tuple-element.6) | data formatting | bytes 4194304
